TPU v7x, 128 devices: a whole 4x4x4 slice. The times are simulated.
128 devices in a mesh: px: 8 (over y_lo, x), py: 16 (over z, y_hi, core).
Axes of the slice: x: 4, y: 4 (y_hi: 2, y_lo: 2; y = y_hi * 2 + y_lo), z: 4, core: 2. Of those that a mesh axis runs over, the one named last changes fastest.
Arguments:
- photons: float32 [4096, 128], P(('px', 'py')), may hold values from 50 to 1000
- halo_cells: int32 [4096, 128], P(('px', 'py')), may hold values from 0 to 442367
- halo_counts: int32 [4096], P(('px', 'py')), may hold values from 1 to 128
- owners: int32 [4096, 1], P(('px', 'py')), may hold values from 0 to 15; in each aligned block of 32 rows (0 to 31, 32 to 63, ...) at most 4 rows name the same one
- density: float32 [384, 384, 384], P('px', 'py'), may hold values from 0.02 to 50
Outputs:
- fraction: float32 [384, 384, 384], P('px', 'py')
Inputs may be any that keep to these rules, and one draw needn't show every extreme that they name: The halos of a block all lie in pencil owners[b] of the block's own slab. Among the 32 blocks of one device no owner appears more than 4 times, a bound that some block reaches. Slots at or past halo_counts[b] are not live and carry arbitrary values. `halo_cells`: A cell index within the owner pencil is (x * 24 + y) * 384 + z with x, y, z local to that pencil.
All inputs are finite; a program needn't handle non-finite values.
Results may differ from a plain program's by a relative error of at most 0.0003.
Values sent between devices are 32-bit elements; how exact they have to be, the bound alone decides.
A program may use at most 128 MiB of HBM per device.

v0:
```python
import math

import jax
import jax.numpy as jnp
from jax import lax
from jax.sharding import PartitionSpec as P

NG = 384
SLOTS = 128
CAP = 4
RADIUS = 20


def in_one_piece(arrays, axis, split_dim, concat_dim, along):
    widths = [math.prod(a.shape[along:]) for a in arrays]
    both = jnp.concatenate(
        [a.reshape(*a.shape[:along], w) for a, w in zip(arrays, widths)], axis=along
    )
    out = lax.all_to_all(both, axis, split_axis=split_dim, concat_axis=concat_dim, tiled=True)
    tiles = jnp.split(out, [sum(widths[:k]) for k in range(1, len(widths))], axis=along)
    return tuple((b.reshape(*out.shape[:along], *a.shape[along:]) for a, b in zip(arrays, tiles)))


def side_by_side(arrays, axis, split_dim, concat_dim, along):
    ends, at = ([], 0)
    for a in arrays[:-1]:
        at += a.shape[along]
        ends.append(at)
    both = jnp.concatenate(arrays, axis=along)
    return tuple(
        jnp.split(
            lax.all_to_all(both, axis, split_axis=split_dim, concat_axis=concat_dim, tiled=True),
            ends,
            axis=along,
        )
    )


def product(form, left, right):
    return jnp.einsum(form, left, right, precision=lax.Precision.HIGHEST)


def rotate(form, real_part, imag_part, cos_table, sin_table, direction):
    signed_sin = direction * sin_table
    first = product(form, real_part + imag_part, cos_table)
    second = product(form, real_part, signed_sin - cos_table)
    third = product(form, imag_part, cos_table + signed_sin)
    return (first - third, first + second)


def tables(length):
    index_row = jnp.arange(length, dtype=jnp.int32)
    angle = (index_row[:, None] * index_row[None, :] % length).astype(jnp.float32) * (
        2.0 * jnp.pi / length
    )
    return (jnp.cos(angle), jnp.sin(angle))


def signed_frequency(index_values):
    return jnp.where(index_values < NG // 2, index_values, index_values - NG).astype(jnp.float32)


def top_hat(freq_x, freq_y, freq_z):
    radial = jnp.sqrt(freq_x * freq_x + freq_y * freq_y + freq_z * freq_z) * (
        2.0 * jnp.pi * RADIUS / NG
    )
    safe = jnp.where(radial > 0, radial, 1.0)
    value = 3.0 * (jnp.sin(safe) - safe * jnp.cos(safe)) / (safe * safe * safe)
    return jnp.where(radial > 0, value, 1.0)


def paint(photon_rows, cell_rows, live_rows, cell_total):
    weights = jnp.where(live_rows, photon_rows, 0.0)
    empty = jnp.zeros((cell_total,), jnp.float32)
    return empty.at[cell_rows.reshape(-1)].add(weights.reshape(-1))


def on_device(photons, halo_cells, halo_counts, owners, density):
    rows_x, rows_y = (density.shape[0], density.shape[1])
    cell_total = rows_x * rows_y * NG
    count_x = lax.axis_size("px")
    count_y = lax.axis_size("py")
    slot_index = jnp.arange(SLOTS, dtype=jnp.int32)[None, :]
    block_count = photons.shape[0]
    target = owners[:, 0]
    one_hot = (target[:, None] == jnp.arange(count_y, dtype=jnp.int32)[None, :]).astype(jnp.int32)
    slot_rank = jnp.sum(jnp.cumsum(one_hot, axis=0) * one_hot, axis=1) - 1
    position = target * CAP + slot_rank
    placing = position[None, :] == jnp.arange(count_y * CAP, dtype=jnp.int32)[:, None]
    source = jnp.sum(
        jnp.where(placing, jnp.arange(block_count, dtype=jnp.int32)[None, :], 0), axis=1
    )
    filled = jnp.any(placing, axis=1)
    send_photons = photons[source]
    send_cells = halo_cells[source]
    send_counts = jnp.where(filled, halo_counts[source], 0)
    got_photons, got_cells, got_counts = (
        lax.all_to_all(send_photons, "py", split_axis=0, concat_axis=0, tiled=True),
        *in_one_piece((send_cells, send_counts), "py", 0, 0, 1),
    )
    live_rows = slot_index < got_counts[:, None]
    painted = paint(got_photons, got_cells, live_rows, cell_total)
    cos_full, sin_full = tables(NG)
    field_rows = painted.reshape(rows_x * rows_y, NG)
    density_rows = density.reshape(rows_x * rows_y, NG)
    spec_real, spec_imag = rotate("az,zk->ka", field_rows, density_rows, cos_full, sin_full, -1.0)
    cos_y = cos_full.reshape(count_y, rows_y, NG)
    sin_y = sin_full.reshape(count_y, rows_y, NG)
    cos_x = cos_full.reshape(count_x, rows_x, NG)
    sin_x = sin_full.reshape(count_x, rows_x, NG)
    freq_all = signed_frequency(jnp.arange(NG, dtype=jnp.int32))
    devices_all = count_x * count_y
    slab_planes = NG // devices_all
    sent = (
        spec_real.reshape(devices_all, slab_planes, rows_x * rows_y),
        spec_imag.reshape(devices_all, slab_planes, rows_x * rows_y),
    )
    got_real, got_imag = side_by_side((sent[0], sent[1]), ("px", "py"), 0, 2, 1)
    got_real = got_real.reshape(slab_planes, count_x, count_y, rows_x, rows_y)
    got_imag = got_imag.reshape(slab_planes, count_x, count_y, rows_x, rows_y)
    plane_real, plane_imag = rotate("kiqxl,qlm->kixm", got_real, got_imag, cos_y, sin_y, -1.0)
    full_real, full_imag = rotate("kixm,ixn->kmn", plane_real, plane_imag, cos_x, sin_x, -1.0)
    freq_z = signed_frequency(
        lax.axis_index(("px", "py")) * slab_planes + jnp.arange(slab_planes, dtype=jnp.int32)
    )
    window = top_hat(freq_z[:, None, None], freq_all[None, :, None], freq_all[None, None, :])
    full_real = full_real * window
    full_imag = full_imag * window
    plane_real, plane_imag = rotate("kmn,ixn->kmix", full_real, full_imag, cos_x, sin_x, 1.0)
    back_real, back_imag = rotate("kmix,qlm->iqkxl", plane_real, plane_imag, cos_y, sin_y, 1.0)
    sent = (
        back_real.reshape(devices_all, slab_planes, rows_x * rows_y),
        back_imag.reshape(devices_all, slab_planes, rows_x * rows_y),
    )
    got_real, got_imag = side_by_side((sent[0], sent[1]), ("px", "py"), 0, 1, 2)
    got_real = got_real.reshape(NG, rows_x * rows_y)
    got_imag = got_imag.reshape(NG, rows_x * rows_y)
    final_real, final_imag = rotate("ka,kz->az", got_real, got_imag, cos_full, sin_full, 1.0)
    scale = 1.0 / (float(NG) * float(NG) * float(NG))
    photon_smooth = final_real * scale
    density_smooth = final_imag * scale
    fraction = jnp.clip(photon_smooth / jnp.maximum(density_smooth, 0.5), 0.0, 1.0)
    return fraction.reshape(rows_x, rows_y, NG)


def solution(mesh):
    placed = (
        P(("px", "py"), None),
        P(("px", "py"), None),
        P(("px", "py")),
        P(("px", "py"), None),
        P("px", "py", None),
    )
    return jax.shard_map(
        on_device, mesh=mesh, in_specs=placed, out_specs=P("px", "py", None), check_vma=False
    )
```

profile of v0, /device:TPU:1, one launch (start us, length us, event | category | flops | bytes accessed | tf_op | source)
XLA Modules:
  0.0 462.9 jit_solution(1115859090516122004)
XLA Ops:
  0.0 0.0 copy-start
  0.0 0.7 fusion.192
  0.7 0.1 reduce_window_sum.11
  0.8 0.8 select_reduce_fusion.1
  1.6 0.7 add_add_fusion
  2.3 0.1 select_reduce_fusion
  2.4 0.1 fusion.191
  2.5 1.4 gather_fusion.1
  3.9 0.2 select_n.133
  4.1 0.0 copy-done
  4.1 0.6 gather_fusion
  4.7 0.6 pad_add_fusion
  5.4 9.4 %all-to-all-start = ((s32[16,4,129]{2,1,0:T(4,128)}), s32[16,4,129]{2,1,0:T(4,128)S(1)}, u32[]{:S(2)}, u32[]{:S(2)}) async-start(s32[16,4,129]{2,1,0:T(4,128)} %pad_add_fusion), calls=%async_computation | async-start | bytes 131072 | tf_op jit(solution)/shard_map/all_to_all | solution.py:19
  14.8 1.9 gather_fusion.2
  16.7 5.4 %all-to-all-done = s32[16,4,129]{2,1,0:T(4,128)S(1)} async-done(((s32[16,4,129]{2,1,0:T(4,128)}), s32[16,4,129]{2,1,0:T(4,128)S(1)}, u32[]{:S(2)}, u32[]{:S(2)}) %all-to-all-start) | async-done | bytes 33056 | tf_op jit(solution)/shard_map/all_to_all | solution.py:19
  22.1 3.7 all-to-all-start.1
  25.9 0.1 slice_reduce_fusion
  26.1 7.2 %all-to-all-done.1 = f32[16,4,128]{2,1,0:T(4,128)S(1)} async-done(((f32[16,4,128]{2,1,0:T(4,128)}), f32[16,4,128]{2,1,0:T(4,128)S(1)}, u32[]{:S(2)}, u32[]{:S(2)}) %all-to-all-start.1) | async-done | bytes 32800 | tf_op jit(solution)/shard_map/all_to_all | solution.py:98
  33.2 0.1 fusion.190
  33.3 43.6 %scatter_custom_fusion = f32[442368]{0:T(1024)S(1)} fusion(s32[8192]{0:T(1024)S(1)} %bitcast.157, f32[8192]{0:T(1024)S(1)} %fusion.190, f32[]{:T(128)} %constant.24.clone.1), kind=kCustom, calls=%fused_computation.55 | custom fusion | flops 8192 | bytes 1769476 | tf_op jit(solution)/shard_map/scatter-add | solution.py:75
  76.9 0.4 reshape.227
  77.3 8.5 %fusion.29 = f32[384,1152]{1,0:T(8,128)S(1)} fusion(f32[1152,384]{1,0:T(8,128)S(1)} %reshape.227, f32[1152,384]{1,0:T(8,128)} %bitcast.152), kind=kOutput, calls=%fused_computation.51 | convolution fusion | flops 2040201216 | bytes 5308416 | tf_op jit(solution)/shard_map/az,zk->ka/dot_general | solution.py:40
  85.9 0.0 copy-start.3
  85.9 9.2 %convolution_add_fusion.1 = f32[384,1152]{1,0:T(8,128)} fusion(f32[384,1152]{1,0:T(8,128)S(1)} %fusion.29, f32[1152,384]{1,0:T(8,128)S(1)} %reshape.227), kind=kOutput, calls=%fused_computation.15 | convolution fusion | flops 2040496128 | bytes 5308416 | tf_op jit(solution)/shard_map/az,zk->ka/dot_general | solution.py:40
  95.1 0.0 copy-done.3
  95.1 8.9 %convolution_subtract_fusion.1 = f32[384,1152]{1,0:T(8,128)} fusion(f32[384,1152]{1,0:T(8,128)S(1)} %fusion.29, f32[1152,384]{1,0:T(8,128)S(1)} %bitcast.153), kind=kOutput, calls=%fused_computation.16 | convolution fusion | flops 2040496128 | bytes 5308416 | tf_op jit(solution)/shard_map/az,zk->ka/dot_general | solution.py:40
  103.9 2.6 reshape.230
  106.6 3.8 reshape.229
  110.4 4.7 %pad_maximum_fusion = f32[128,6,1152]{2,1,0:T(8,128)} fusion(f32[128,3,1152]{2,1,0:T(4,128)S(1)} %reshape.230, f32[128,3,1152]{2,1,0:T(4,128)} %reshape.229), kind=kLoop, calls=%fused_computation.6 | loop fusion | flops 884736 | bytes 7077888 | tf_op jit(solution)/shard_map/concatenate | solution.py:29
  115.1 5.5 %all-to-all-start.2 = ((f32[128,6,1152]{2,1,0:T(8,128)}), f32[128,6,1152]{2,1,0:T(8,128)}, u32[]{:S(2)}, u32[]{:S(2)}) async-start(f32[128,6,1152]{2,1,0:T(8,128)} %pad_maximum_fusion), calls=%async_computation.2 | async-start | bytes 9437184 | tf_op jit(solution)/shard_map/all_to_all | solution.py:32
  120.6 0.1 broadcast_add_fusion
  120.7 60.3 %all-to-all-done.2 = f32[128,6,1152]{2,1,0:T(8,128)} async-done(((f32[128,6,1152]{2,1,0:T(8,128)}), f32[128,6,1152]{2,1,0:T(8,128)}, u32[]{:S(2)}, u32[]{:S(2)}) %all-to-all-start.2) | async-done | bytes 3538976 | tf_op jit(solution)/shard_map/all_to_all | solution.py:32
  181.1 6.1 %fusion.258 = (f32[1,3,147456]{2,1,0:T(4,128)S(1)}, f32[1,3,147456]{2,1,0:T(4,128)}) fusion(f32[1,6,147456]{2,1,0:T(8,128)} %bitcast.14), kind=kLoop, calls=%fused_computation.251 | loop fusion | bytes 7077888 | tf_op jit(solution)/shard_map/split | solution.py:31
  187.2 12.4 %reshape.231 = f32[3,8,16,48,24]{4,3,2,1,0:T(8,128)} reshape(f32[1,3,147456]{2,1,0:T(4,128)} %get-tuple-element.6) | data formatting | bytes 3538944 | tf_op jit(solution)/shard_map/reshape | solution.py:119
  199.6 10.9 %reshape.232 = f32[3,8,16,48,24]{4,3,2,1,0:T(8,128)} reshape(f32[1,3,147456]{2,1,0:T(4,128)S(1)} %get-tuple-element.5) | data formatting | bytes 3538944 | tf_op jit(solution)/shard_map/reshape | solution.py:120
  210.4 17.2 %fusion = f32[3,8,48,384,1]{3,2,4,1,0:T(8,128)S(1)} fusion(f32[3,8,16,48,24]{4,3,2,1,0:T(8,128)} %reshape.231, f32[3,8,16,48,24]{4,3,2,1,0:T(8,128)} %reshape.232, s32[16,24]{1,0:T(8,128)S(1)} %multiply_add_fusion), kind=kOutput, calls=%fused_computation.4 | convolution fusion | flops 2040201216 | bytes 5309952 | tf_op jit(solution)/shard_map/kiqxl,qlm->kixm/dot_general | solution.py:40
  227.7 0.0 copy-done.2
  227.7 0.0 slice-start.2
  227.7 10.6 %bitcast_add_fusion.1 = f32[3,8,48,384]{3,2,1,0:T(8,128)S(1)} fusion(f32[3,8,48,384,1]{3,2,4,1,0:T(8,128)S(1)} %fusion, f32[3,8,16,48,24]{4,3,2,1,0:T(8,128)S(1)} %copy-done.2, s32[16,24]{1,0:T(8,128)S(1)} %multiply_add_fusion), kind=kOutput, calls=%fused_computation.43 | convolution fusion | flops 2040496128 | bytes 5309952 | tf_op jit(solution)/shard_map/kiqxl,qlm->kixm/dot_general | solution.py:40
  238.3 0.0 slice-done
  238.3 0.0 slice-done.1
  238.3 11.0 %bitcast_subtract_fusion.1 = f32[3,8,48,384]{3,2,1,0:T(8,128)S(1)} fusion(f32[3,8,48,384,1]{3,2,4,1,0:T(8,128)S(1)} %fusion, f32[3,8,16,48,24]{4,3,2,1,0:T(8,128)S(1)} %bitcast.151, s32[16,24]{1,0:T(8,128)S(1)} %multiply_add_fusion), kind=kOutput, calls=%fused_computation.44 | convolution fusion | flops 2040496128 | bytes 5309952 | tf_op jit(solution)/shard_map/kiqxl,qlm->kixm/dot_general | solution.py:40
  249.3 6.1 %fusion.27 = f32[3,384,384,1]{2,1,3,0:T(8,128)S(1)} fusion(f32[3,8,48,384]{3,2,1,0:T(8,128)S(1)} %bitcast_subtract_fusion.1, f32[3,8,48,384]{3,2,1,0:T(8,128)S(1)} %bitcast_add_fusion.1, s32[8,48]{1,0:T(8,128)S(1)} %multiply_add_fusion.1), kind=kOutput, calls=%fused_computation.49 | convolution fusion | flops 2040201216 | bytes 5309952 | tf_op jit(solution)/shard_map/kixm,ixn->kmn/dot_general | solution.py:40
  255.5 13.6 %fusion.21 = f32[3,384,384]{2,1,0:T(8,128)S(1)} fusion(f32[3,384,384,1]{2,1,3,0:T(8,128)S(1)} %fusion.27, f32[3,8,48,384]{3,2,1,0:T(8,128)S(1)} %bitcast_subtract_fusion.1, f32[384]{0:T(512)S(1)} %fusion.194, f32[3,384]{1,0:T(4,128)S(1)} %broadcast_add_fusion, s32[8,48]{1,0:T(8,128)S(1)} %multiply_add_fusion.1), kind=kOutput, calls=%fused_computation.40 | convolution fusion | flops 2045804544 | bytes 5316096 | tf_op jit(solution)/shard_map/kixm,ixn->kmn/dot_general | solution.py:40
  269.0 13.7 %fusion.22 = f32[3,384,384]{2,1,0:T(8,128)S(1)} fusion(f32[3,384,384,1]{2,1,3,0:T(8,128)S(1)} %fusion.27, f32[3,8,48,384]{3,2,1,0:T(8,128)S(1)} %bitcast_add_fusion.1, f32[384]{0:T(512)S(1)} %fusion.194, f32[3,384]{1,0:T(4,128)S(1)} %broadcast_add_fusion, s32[8,48]{1,0:T(8,128)S(1)} %multiply_add_fusion.1), kind=kOutput, calls=%fused_computation.42 | convolution fusion | flops 2045804544 | bytes 5316096 | tf_op jit(solution)/shard_map/kixm,ixn->kmn/dot_general | solution.py:40
  282.7 5.8 %fusion.15 = f32[3,384,8,48]{1,3,2,0:T(8,128)S(1)} fusion(f32[3,384,384]{2,1,0:T(8,128)S(1)} %fusion.22, f32[3,384,384]{2,1,0:T(8,128)S(1)} %fusion.21, s32[8,48]{1,0:T(8,128)S(1)} %multiply_add_fusion.1), kind=kOutput, calls=%fused_computation.33 | convolution fusion | flops 2040201216 | bytes 5309952 | tf_op jit(solution)/shard_map/kmn,ixn->kmix/dot_general | solution.py:40
  288.5 5.8 %fusion.34 = f32[3,384,8,48]{1,3,2,0:T(8,128)S(1)} fusion(f32[3,384,8,48]{1,3,2,0:T(8,128)S(1)} %fusion.15, f32[3,384,384]{2,1,0:T(8,128)S(1)} %fusion.22, s32[8,48]{1,0:T(8,128)S(1)} %multiply_add_fusion.1), kind=kOutput, calls=%fused_computation.54 | convolution fusion | flops 2040348672 | bytes 5309952 | tf_op jit(solution)/shard_map/kmn,ixn->kmix/dot_general | solution.py:40
  294.3 5.8 %fusion.31 = f32[3,384,8,48]{1,3,2,0:T(8,128)S(1)} fusion(f32[3,384,8,48]{1,3,2,0:T(8,128)S(1)} %fusion.15, f32[3,384,384]{2,1,0:T(8,128)S(1)} %fusion.21, s32[8,48]{1,0:T(8,128)S(1)} %multiply_add_fusion.1), kind=kOutput, calls=%fused_computation.53 | convolution fusion | flops 2040348672 | bytes 5309952 | tf_op jit(solution)/shard_map/kmn,ixn->kmix/dot_general | solution.py:40
  300.1 10.3 %fusion.19 = f32[16,24,3,8,48]{4,1,3,2,0:T(8,128)S(1)} fusion(f32[3,384,8,48]{1,3,2,0:T(8,128)S(1)} %fusion.31, f32[3,384,8,48]{1,3,2,0:T(8,128)S(1)} %fusion.34, s32[16,24]{1,0:T(8,128)S(1)} %multiply_add_fusion), kind=kOutput, calls=%fused_computation.37 | convolution fusion | flops 2040201216 | bytes 5309952 | tf_op jit(solution)/shard_map/kmix,qlm->iqkxl/dot_general | solution.py:40
  310.4 13.7 %subtract_bitcast_fusion = f32[8,16,3,48,24]{3,4,0,2,1:T(8,128)} fusion(f32[16,24,3,8,48]{4,1,3,2,0:T(8,128)S(1)} %fusion.19, f32[3,384,8,48]{1,3,2,0:T(8,128)S(1)} %fusion.34, s32[16,24]{1,0:T(8,128)S(1)} %multiply_add_fusion), kind=kOutput, calls=%fused_computation.8 | convolution fusion | flops 2040348672 | bytes 5309952 | tf_op jit(solution)/shard_map/kmix,qlm->iqkxl/dot_general | solution.py:40
  324.1 11.8 %add_bitcast_fusion = f32[8,16,3,48,24]{3,4,0,2,1:T(8,128)} fusion(f32[16,24,3,8,48]{4,1,3,2,0:T(8,128)S(1)} %fusion.19, f32[3,384,8,48]{1,3,2,0:T(8,128)S(1)} %fusion.31, s32[16,24]{1,0:T(8,128)S(1)} %multiply_add_fusion), kind=kOutput, calls=%fused_computation.7 | convolution fusion | flops 2040348672 | bytes 5309952 | tf_op jit(solution)/shard_map/kmix,qlm->iqkxl/dot_general | solution.py:40
  336.0 8.2 %copy.33 = f32[8,16,3,48,24]{4,3,1,0,2:T(8,128)} copy(f32[8,16,3,48,24]{3,4,0,2,1:T(8,128)} %subtract_bitcast_fusion) | data formatting | bytes 3538944 | tf_op jit(solution)/shard_map/sub | solution.py:48
  344.1 7.4 %reshape.233 = f32[128,3,1152]{2,0,1:T(8,128)S(1)} reshape(f32[8,16,3,48,24]{4,3,1,0,2:T(8,128)} %copy.33) | data formatting | bytes 3538944 | tf_op jit(solution)/shard_map/reshape | solution.py:132
  351.5 8.2 %copy.34 = f32[8,16,3,48,24]{4,3,1,0,2:T(8,128)} copy(f32[8,16,3,48,24]{3,4,0,2,1:T(8,128)} %add_bitcast_fusion) | data formatting | bytes 3538944 | tf_op jit(solution)/shard_map/add | solution.py:48
  359.7 7.4 %reshape.234 = f32[128,3,1152]{2,0,1:T(8,128)S(1)} reshape(f32[8,16,3,48,24]{4,3,1,0,2:T(8,128)} %copy.34) | data formatting | bytes 3538944 | tf_op jit(solution)/shard_map/reshape | solution.py:133
  367.0 0.3 pad_maximum_fusion.1
  367.3 2.4 copy.35
  369.8 68.1 %all_to_all.51 = f32[128,3,2304]{2,1,0:T(4,128)} all-to-all(f32[128,3,2304]{2,1,0:T(4,128)S(1)} %copy.35), channel_id=1, replica_groups=mesh['px'=8,'py'=16] {'px','py'}, dimensions={0} | all-to-all | bytes 7077888 | tf_op jit(solution)/shard_map/all_to_all | solution.py:32
  437.9 4.9 %all_to_all.46 = f32[1,384,2304]{2,1,0:T(8,128)S(1)} reshape(f32[128,3,2304]{2,1,0:T(4,128)} %all_to_all.51) | data formatting | bytes 7077888 | tf_op jit(solution)/shard_map/all_to_all | solution.py:32
  442.8 5.8 %fusion.23 = f32[1152,384]{1,0:T(8,128)S(1)} fusion(f32[1,384,2304]{2,1,0:T(8,128)S(1)} %all_to_all.46), kind=kOutput, calls=%fused_computation.45 | convolution fusion | flops 2040201216 | bytes 5308416 | tf_op jit(solution)/shard_map/ka,kz->az/dot_general | solution.py:40
  448.7 6.2 %fusion.3 = f32[1152,384]{1,0:T(8,128)S(1)} fusion(f32[1152,384]{1,0:T(8,128)S(1)} %fusion.23, f32[1,384,2304]{2,1,0:T(8,128)S(1)} %all_to_all.46), kind=kOutput, calls=%fused_computation.12 | convolution fusion | flops 2041233408 | bytes 5308416 | tf_op jit(solution)/shard_map/ka,kz->az/dot_general | solution.py:40
  454.8 0.0 copy-start.1
  454.8 7.6 %fusion.6 = f32[1152,384]{1,0:T(8,128)} fusion(f32[1152,384]{1,0:T(8,128)S(1)} %fusion.3, f32[1152,384]{1,0:T(8,128)S(1)} %fusion.23, f32[1,384,2304]{2,1,0:T(8,128)S(1)} %all_to_all.46), kind=kOutput, calls=%fused_computation.18 | convolution fusion | flops 2041675776 | bytes 7077888 | tf_op jit(solution)/shard_map/ka,kz->az/dot_general | solution.py:40
  462.4 0.0 copy-done.1
  (15 shorter events, 0.1 us)
Async XLA Ops:
  0.0 4.1 copy-start
  5.4 16.8 %all-to-all-start = ((s32[16,4,129]{2,1,0:T(4,128)}), s32[16,4,129]{2,1,0:T(4,128)S(1)}, u32[]{:S(2)}, u32[]{:S(2)}) async-start(s32[16,4,129]{2,1,0:T(4,128)} %pad_add_fusion), calls=%async_computation | async-start | bytes 131072 | tf_op jit(solution)/shard_map/all_to_all | solution.py:19
  22.1 11.1 %all-to-all-start.1 = ((f32[16,4,128]{2,1,0:T(4,128)}), f32[16,4,128]{2,1,0:T(4,128)S(1)}, u32[]{:S(2)}, u32[]{:S(2)}) async-start(f32[16,4,128]{2,1,0:T(4,128)} %bitcast.9), calls=%async_computation.1 | async-start | bytes 65536 | tf_op jit(solution)/shard_map/all_to_all | solution.py:98
  85.9 9.2 %copy-start.3 = (f32[48,24,384]{2,1,0:T(8,128)S(1)}, f32[48,24,384]{2,1,0:T(8,128)}, u32[]{:S(2)}) copy-start(f32[48,24,384]{2,1,0:T(8,128)} %param.9) | copy-start | bytes 5308420
  115.1 65.9 %all-to-all-start.2 = ((f32[128,6,1152]{2,1,0:T(8,128)}), f32[128,6,1152]{2,1,0:T(8,128)}, u32[]{:S(2)}, u32[]{:S(2)}) async-start(f32[128,6,1152]{2,1,0:T(8,128)} %pad_maximum_fusion), calls=%async_computation.2 | async-start | bytes 9437184 | tf_op jit(solution)/shard_map/all_to_all | solution.py:32
  210.4 17.2 %copy-start.2 = (f32[3,8,16,48,24]{4,3,2,1,0:T(8,128)S(1)}, f32[3,8,16,48,24]{4,3,2,1,0:T(8,128)}, u32[]{:S(2)}) copy-start(f32[3,8,16,48,24]{4,3,2,1,0:T(8,128)} %reshape.231) | copy-start | bytes 5308420
  210.4 27.9 %slice-start = ((s8[9437184]{0:T(1024)(128)(4,1)}), s8[4194304]{0:T(1024)(128)(4,1)S(1)}, s32[]{:S(2)}) async-start(s8[9437184]{0:T(1024)(128)(4,1)} %bitcast.150), calls=%async_computation.4 | async-start | bytes 8388608
  210.4 27.9 %slice-start.1 = ((s8[9437184]{0:T(1024)(128)(4,1)}), s8[4194304]{0:T(1024)(128)(4,1)S(1)}, s32[]{:S(2)}) async-start(s8[9437184]{0:T(1024)(128)(4,1)} %bitcast.150), calls=%async_computation.5 | async-start | bytes 8388608
  227.7 10.7 %slice-start.2 = ((s8[9437184]{0:T(1024)(128)(4,1)}), s8[1048576]{0:T(1024)(128)(4,1)S(1)}, s32[]{:S(2)}) async-start(s8[9437184]{0:T(1024)(128)(4,1)} %bitcast.150), calls=%async_computation.6 | async-start | bytes 2097152
  454.8 7.6 %copy-start.1 = (s32[32,128]{1,0:T(8,128)S(1)}, s32[32,128]{1,0:T(8,128)}, u32[]{:S(2)}) copy-start(s32[32,128]{1,0:T(8,128)} %param.6) | copy-start | bytes 49156
where the time goes:
time: 472 us; the launch traced here: 463 us
  matrix products  172 us (36%)
  local copies, waits for them, and re-layouts  78.9 us (17%)
  waiting for transfers between devices  72.9 us (15%)
  blocking collectives  68.1 us (14%)
  other arithmetic  52 us (11%)
  starting transfers between devices  18.6 us (4%)
    dot_general x18, matrix products, product(): return jnp.einsum(form, left, right, precision=lax.Precision.HIGHEST)  172 us
    all_to_all x1, blocking collectives, side_by_side(): lax.all_to_all(both, axis, split_axis=split_dim, concat_axis=concat_dim,...  68.1 us
    all_to_all x1, waiting for transfers between devices, side_by_side(): lax.all_to_all(both, axis, split_axis=split_dim, concat_axis=concat_dim,...  60.3 us
    scatter-add x1, other arithmetic, paint(): return empty.at[cell_rows.reshape(-1)].add(weights.reshape(-1))  43.6 us
    reshape x1, local copies, waits for them, and re-layouts, on_device(): got_real = got_real.reshape(slab_planes, count_x, count_y, rows_x, rows_y)  12.4 us
    reshape x1, local copies, waits for them, and re-layouts, on_device(): got_imag = got_imag.reshape(slab_planes, count_x, count_y, rows_x, rows_y)  10.9 us
    all_to_all x1, starting transfers between devices, in_one_piece(): lax.all_to_all(both, axis, split_axis=split_dim, concat_axis=concat_dim,...  9.45 us
  transfers between devices with their start and end apart: 3, of which 3 were waited for; matrix products, arithmetic and copies ran while one was open for 0% of the time, Pallas kernels for 0%

commit v1 on v0

v1 whole, which is shorter than its diff:
```python
import functools

import jax
import jax.numpy as jnp
import numpy as np
from jax import lax
from jax.experimental import pallas as pl
from jax.experimental.pallas import tpu as pltpu
from jax.sharding import PartitionSpec as P

NG = 384
SLOTS = 128
CAP = 4
RADIUS = 20
DEV = 128
CELLS = 1152
PLANE = 2 * CELLS
HEAD = 72
TAIL = 56
LIMIT = 60 * 1024 * 1024
F32 = jnp.float32
BF16 = jnp.bfloat16
VMEM = pltpu.VMEM
SMEM = pltpu.SMEM


def cut(v):
    hi = v.astype(BF16)
    return hi, (v - hi.astype(F32)).astype(BF16)


def cut_np(v):
    v = np.asarray(v, np.float32)
    hi = v.astype(jnp.bfloat16)
    lo = (v - hi.astype(np.float32)).astype(jnp.bfloat16)
    return hi, lo


NN = (((1,), (0,)), ((), ()))
NT = (((1,), (1,)), ((), ()))


def mm(a, b, dims):
    return lax.dot_general(a, b, dims, preferred_element_type=F32)


def mm3(ah, al, bh, bl, dims=NN):
    return mm(ah, bh, dims) + (mm(ah, bl, dims) + mm(al, bh, dims))


def kz_first():
    return np.arange(1, DEV + 1)


def kz_second():
    k = np.zeros(DEV, np.int64)
    k[:63] = 129 + np.arange(63)
    k[63] = 0
    k[64] = NG // 2
    k[65:] = 129 + np.arange(63)
    return k


def z_tables():
    z = np.arange(NG)

    def c(k):
        return np.cos(2 * np.pi * ((k[:, None] * z[None]) % NG) / NG)

    def s(k):
        return np.sin(2 * np.pi * ((k[:, None] * z[None]) % NG) / NG)

    first = np.concatenate([c(kz_first()), s(kz_first())])
    k = kz_second()
    d = np.arange(DEV)[:, None]
    special = (d == 63) | (d == 64)
    g_re = np.where(d < 63, c(k), 0.0)
    g_im = np.where(d < 63, s(k), 0.0) + np.where(special, c(k), 0.0)
    f_re = np.where(d > 62, c(k), 0.0)
    f_im = np.where(d > 64, s(k), 0.0)
    second_g = np.concatenate([g_re[:HEAD], g_im[:HEAD]])
    second_f = np.concatenate([f_re[TAIL:], f_im[TAIL:]])
    return first, second_g, second_f


def mix(left, right):
    i = np.arange(left * right)
    a, b = i // right, i % right
    ph = -2j * np.pi * (np.outer(a, a) / left + np.outer(b, b) / right)
    return np.exp(ph)


def row_matrix(sign):
    m = mix(8, 16)
    re, im = m.real, sign * m.imag
    return np.block([[re, -im], [im, re]])


def lane_matrix(sign):
    m = mix(16, 8)
    re, im = m.real, sign * m.imag
    return np.block([[re, im], [-im, re]])


def freq_parts():
    row = lax.broadcasted_iota(jnp.int32, (CELLS, 128), 0)
    lane = lax.broadcasted_iota(jnp.int32, (CELLS, 128), 1)
    m, s = row // 128, row % 128
    return s // 16, s % 16, m // 3, m % 3, lane // 8, lane % 8


def twiddles():
    ax, ay, bx, by, cx, cy = freq_parts()
    w = 2.0 * jnp.pi / NG
    one = ((ax * bx * 16 + ay * by * 8) % NG).astype(F32) * w
    two = ((cx * (ax + 8 * bx) + cy * (ay + 16 * by)) % NG).astype(F32) * w
    return jnp.cos(one), -jnp.sin(one), jnp.cos(two), -jnp.sin(two)


def signed(k):
    return jnp.where(k < NG // 2, k, k - NG).astype(F32)


def top_hat(freq_x, freq_y, freq_z):
    radial = jnp.sqrt(freq_x * freq_x + freq_y * freq_y + freq_z * freq_z) * (2.0 * jnp.pi * RADIUS / NG)
    safe = jnp.where(radial > 0, radial, 1.0)
    value = 3.0 * (jnp.sin(safe) - safe * jnp.cos(safe)) / (safe * safe * safe)
    return jnp.where(radial > 0, value, 1.0)


def window(me, kz):
    ax, ay, bx, by, cx, cy = freq_parts()
    kx, ky = ax + 8 * bx + 24 * cx, ay + 16 * by + 48 * cy
    k = jnp.asarray(kz, jnp.int32)[me]
    scale = jnp.where((k == 0) | (k == NG // 2), 1.0, 2.0) / float(NG) ** 3
    return top_hat(signed(kx), signed(ky), signed(k)) * scale


def call(body, out_shape, args, scratch, spaces=None, flops=0, nbytes=0, name=None, **params):
    spaces = spaces or [VMEM] * len(args)
    outs = jax.tree.map(lambda _: pl.BlockSpec(memory_space=VMEM), out_shape)
    return pl.pallas_call(
        body,
        out_shape=out_shape,
        in_specs=[pl.BlockSpec(memory_space=s) for s in spaces],
        out_specs=outs,
        scratch_shapes=scratch,
        compiler_params=pltpu.CompilerParams(vmem_limit_bytes=LIMIT, **params),
        cost_estimate=pl.CostEstimate(flops=flops, bytes_accessed=nbytes, transcendentals=0),
        name=name,
    )(*args)


def prep_body(ph_ref, cell_ref, count_ref, own_col, own_row, out_ref):
    lane = lax.broadcasted_iota(jnp.int32, (32, SLOTS), 1)
    live = lane < count_ref[...]
    w = jnp.where(live, ph_ref[...], 0.0)
    cells = jnp.where(live, cell_ref[...], 0).astype(F32)
    before = lax.broadcasted_iota(jnp.int32, (32, 32), 0) < lax.broadcasted_iota(jnp.int32, (32, 32), 1)
    same = (own_col[...] == own_row[...]) & before
    rank = jnp.sum(jnp.where(same, 1.0, 0.0), axis=0, keepdims=True).astype(jnp.int32)
    place = own_row[...] * (2 * CAP) + rank
    rows = lax.broadcasted_iota(jnp.int32, (DEV, 32), 0)
    total = jnp.zeros((DEV, SLOTS), F32)
    for values, shift in ((w, 0), (cells, CAP)):
        hot = jnp.where(rows == place + shift, 1.0, 0.0).astype(BF16)
        hi = values.astype(BF16)
        rest = values - hi.astype(F32)
        mid = rest.astype(BF16)
        low = (rest - mid.astype(F32)).astype(BF16)
        total = total + ((mm(hot, hi, NN) + mm(hot, mid, NN)) + mm(hot, low, NN))
    out_ref[...] = total.reshape(16, 2 * CAP, SLOTS)


def density_body(dens, t0h, t0l, t1h, t1l, x0, y1, gh, gl):
    for m in range(9):
        xh, lh = m // 3, m % 3
        rows = [dens[(16 * xh + xl) * 24 + 8 * lh : (16 * xh + xl) * 24 + 8 * lh + 8, :] for xl in range(16)]
        hi, lo = cut(jnp.concatenate(rows, axis=0))
        gh[m * 128 : (m + 1) * 128, :] = hi
        gl[m * 128 : (m + 1) * 128, :] = lo
    res = mm3(t0h[...], t0l[...], gh[...], gl[...], NT)
    x0[:, 0, :CELLS] = res[:DEV]
    x0[:, 0, CELLS:] = res[DEV:]
    y1[...] = mm3(t1h[...], t1l[...], gh[...], gl[...], NT)


BUFS = 4
UNROLL = 8


def paint_body(cnt, idx, ph, t0h, t0l, t1h, t1l, y1, x12, b0, b1, b2, b3, fh, fl):
    bufs = (b0, b1, b2, b3)
    zero = jnp.zeros((128, 128), F32)

    def clear(i, carry):
        at = pl.multiple_of(i * 128, 128)
        for b in bufs:
            b[pl.ds(at, 128), :] = zero
        return carry

    lax.fori_loop(0, 27, clear, 0)
    lane = lax.broadcasted_iota(jnp.int32, (1, 128), 1)

    def one_row(r, carry):
        def step(jb, inner):
            for u in range(UNROLL):
                j = jb * UNROLL + u
                at = idx[r, j]
                b = bufs[u % BUFS]
                row = lax.shift_right_logical(at, 7)
                here = lane == lax.bitwise_and(at, 127)
                b[pl.ds(row, 1), :] = b[pl.ds(row, 1), :] + jnp.where(here, ph[r, j], 0.0)
            return inner

        return lax.fori_loop(0, (cnt[r] + UNROLL - 1) // UNROLL, step, carry)

    lax.fori_loop(0, 16 * CAP, one_row, 0)
    for m in range(9):
        for zc in range(3):
            at = (zc * 9 + m) * 128
            v = (b0[at : at + 128, :] + b1[at : at + 128, :]) + (b2[at : at + 128, :] + b3[at : at + 128, :])
            hi, lo = cut(v)
            fh[m * 128 : (m + 1) * 128, zc * 128 : (zc + 1) * 128] = hi
            fl[m * 128 : (m + 1) * 128, zc * 128 : (zc + 1) * 128] = lo
    part = mm3(t1h[...], t1l[...], fh[...], fl[...], NT)
    for c in range(2):
        x12[:TAIL, 0, c * CELLS : (c + 1) * CELLS] = y1[c * HEAD : c * HEAD + TAIL, :]
        x12[TAIL:HEAD, 0, c * CELLS : (c + 1) * CELLS] = (
            y1[c * HEAD + TAIL : (c + 1) * HEAD, :] + part[c * HEAD : c * HEAD + HEAD - TAIL]
        )
        x12[HEAD:, 0, c * CELLS : (c + 1) * CELLS] = part[c * HEAD + HEAD - TAIL : (c + 1) * HEAD]
    res = mm3(t0h[...], t0l[...], fh[...], fl[...], NT)
    x12[:, 0, PLANE : PLANE + CELLS] = res[:DEV]
    x12[:, 0, PLANE + CELLS :] = res[DEV:]


ROOT = 0.8660254037844386


def three(a, b, c, inverse):
    tr, ti = b[0] + c[0], b[1] + c[1]
    dr, di = ROOT * (b[0] - c[0]), ROOT * (b[1] - c[1])
    er, ei = a[0] - 0.5 * tr, a[1] - 0.5 * ti
    one, two = (er + di, ei - dr), (er - di, ei + dr)
    return (a[0] + tr, a[1] + ti), *((two, one) if inverse else (one, two))


def nine(v, inverse):
    v = list(v)
    for x in range(3):
        v[3 * x : 3 * x + 3] = three(*v[3 * x : 3 * x + 3], inverse)
    for y in range(3):
        v[y], v[y + 3], v[y + 6] = three(v[y], v[y + 3], v[y + 6], inverse)
    return v


def turn(v, c, s):
    return v[0] * c - v[1] * s, v[0] * s + v[1] * c


RB = 16


def planes_body(n, x, w, ah, al, bh, bl, ch, cl, dh, dl, c1, s1, c2, s2, y, wide, tall, uh, ul, vh, vl):
    for p in range(n):
        base = p * PLANE
        for c in range(2):
            wide[c * DEV : (c + 1) * DEV, :] = x[:, 0, base + c * CELLS : base + (c + 1) * CELLS]
        hi, lo = cut(wide[...])
        wide[...] = mm3(ah[...], al[...], hi, lo)

        def forward(i, carry):
            r = pl.multiple_of(i * RB, RB)
            v = []
            for m in range(9):
                cols = slice(m * 128, (m + 1) * 128)
                t = pl.ds(m * 128 + r, RB)
                u = (wide[pl.ds(r, RB), cols], wide[pl.ds(DEV + r, RB), cols])
                v.append(turn(u, c1[t, :], s1[t, :]))
            for m, u in enumerate(nine(v, False)):
                t = pl.ds(m * 128 + r, RB)
                for c, part in enumerate(turn(u, c2[t, :], s2[t, :])):
                    hi, lo = cut(part)
                    uh[t, c * 128 : (c + 1) * 128] = hi
                    ul[t, c * 128 : (c + 1) * 128] = lo
            return carry

        lax.fori_loop(0, DEV // RB, forward, 0)
        mid = mm3(uh[...], ul[...], ch[...], cl[...])
        win = w[p]
        for c in range(2):
            hi, lo = cut(mid[:, c * 128 : (c + 1) * 128] * win)
            uh[:, c * 128 : (c + 1) * 128] = hi
            ul[:, c * 128 : (c + 1) * 128] = lo
        tall[...] = mm3(uh[...], ul[...], dh[...], dl[...])

        def backward(i, carry):
            r = pl.multiple_of(i * RB, RB)
            v = []
            for m in range(9):
                t = pl.ds(m * 128 + r, RB)
                v.append(turn((tall[t, :128], tall[t, 128:]), c2[t, :], -s2[t, :]))
            for m, u in enumerate(nine(v, True)):
                t = pl.ds(m * 128 + r, RB)
                cols = slice(m * 128, (m + 1) * 128)
                for c, part in enumerate(turn(u, c1[t, :], -s1[t, :])):
                    hi, lo = cut(part)
                    vh[pl.ds(c * DEV + r, RB), cols] = hi
                    vl[pl.ds(c * DEV + r, RB), cols] = lo
            return carry

        lax.fori_loop(0, DEV // RB, backward, 0)
        back = mm3(bh[...], bl[...], vh[...], vl[...])
        for c in range(2):
            y[:, 0, base + c * CELLS : base + (c + 1) * CELLS] = back[c * DEV : (c + 1) * DEV]


def last_body(r0, r12, gth, gtl, fth, ftl, out, stack, ga, fa):
    for c in range(2):
        stack[c * DEV : (c + 1) * DEV, :] = r0[:, 0, c * CELLS : (c + 1) * CELLS]
        stack[2 * DEV + c * HEAD : 2 * DEV + (c + 1) * HEAD, :] = r12[:HEAD, 0, c * CELLS : (c + 1) * CELLS]
    hi, lo = cut(stack[...])
    ga[...] = mm3(gth[...], gtl[...], hi, lo)
    for c in range(2):
        stack[c * DEV : (c + 1) * DEV, :] = r12[:, 0, PLANE + c * CELLS : PLANE + (c + 1) * CELLS]
        stack[2 * DEV + c * HEAD : 2 * DEV + (c + 1) * HEAD, :] = r12[TAIL:, 0, c * CELLS : (c + 1) * CELLS]
    hi, lo = cut(stack[...])
    fa[...] = mm3(fth[...], ftl[...], hi, lo)
    for m in range(9):
        xh, lh = m // 3, m % 3
        cols = slice(m * 128, (m + 1) * 128)
        frac = jnp.clip(fa[:, cols] / jnp.maximum(ga[:, cols], 0.5), 0.0, 1.0)
        turned = frac.T
        for xl in range(16):
            at = (16 * xh + xl) * 24 + 8 * lh
            out[at : at + 8, :] = turned[xl * 8 : xl * 8 + 8, :]


def sds(*shape, dtype=F32):
    return jax.ShapeDtypeStruct(shape, dtype)


def exchange(a):
    return lax.all_to_all(a, ("px", "py"), split_axis=0, concat_axis=0, tiled=True)


def planes(x, w, tabs):
    n = w.shape[0]
    return call(
        functools.partial(planes_body, n),
        sds(DEV, 1, n * PLANE),
        (x, w, *tabs),
        [VMEM((256, CELLS), F32), VMEM((CELLS, 256), F32)]
        + [VMEM((CELLS, 256), BF16)] * 2
        + [VMEM((256, CELLS), BF16)] * 2,
        flops=n * 4 * 3 * 2 * 256 * 256 * CELLS,
        nbytes=n * PLANE * DEV * 8,
        name="planes",
    )


def on_device(photons, halo_cells, halo_counts, owners, density):
    first, second_g, second_f = z_tables()
    t0 = [jnp.asarray(t) for t in cut_np(first)]
    t1g = [jnp.asarray(t) for t in cut_np(second_g)]
    t1f = [jnp.asarray(t) for t in cut_np(second_f)]
    back_g = [jnp.asarray(t) for t in cut_np(np.concatenate([first, second_g]).T)]
    back_f = [jnp.asarray(t) for t in cut_np(np.concatenate([first, second_f]).T)]
    mats = []
    for m in (row_matrix(1), row_matrix(-1), lane_matrix(1), lane_matrix(-1)):
        mats += [jnp.asarray(t) for t in cut_np(m)]
    me = lax.axis_index(("px", "py"))

    send = call(
        prep_body,
        sds(16, 2 * CAP, SLOTS),
        (photons, halo_cells, halo_counts.reshape(32, 1), owners, owners.reshape(1, 32)),
        [],
        flops=1 << 20,
        nbytes=1 << 17,
        name="prep",
    )
    got = lax.all_to_all(send, "py", split_axis=0, concat_axis=0, tiled=True)
    x0, y1 = call(
        density_body,
        (sds(DEV, 1, PLANE), sds(2 * HEAD, CELLS)),
        (density.reshape(CELLS, NG), *t0, *t1g),
        [VMEM((CELLS, NG), BF16)] * 2,
        flops=6 * 400 * NG * CELLS,
        nbytes=4 << 20,
        name="density",
    )
    x0 = exchange(x0)
    ph = got[:, :CAP].reshape(16 * CAP, SLOTS)
    cell = got[:, CAP:].reshape(16 * CAP, SLOTS).astype(jnp.int32)
    cnt = jnp.sum((ph > 0).astype(jnp.int32), axis=1)
    gx, gy, gz = cell // (24 * NG), cell // NG % 24, cell % NG
    chunk = gx // 16 * 3 + gy // 8
    idx = (((gz // 128) * 9 + chunk) * 128 + gx % 16 * 8 + gy % 8) * 128 + gz % 128
    x12 = call(
        paint_body,
        sds(DEV, 1, 2 * PLANE),
        (cnt, idx, ph, *t0, *t1f, y1),
        [VMEM((3 * CELLS, 128), F32)] * BUFS + [VMEM((CELLS, NG), BF16)] * 2,
        spaces=[SMEM] * 3 + [VMEM] * 5,
        flops=6 * 400 * NG * CELLS * 3,
        nbytes=4 << 20,
        name="paint",
    )
    x12 = exchange(x12)
    tabs = (*mats, *twiddles())
    r0 = planes(x0, window(me, kz_first())[None], tabs)
    r0 = exchange(r0)
    w12 = jnp.stack([window(me, kz_second()), window(me, kz_first())])
    r12 = exchange(planes(x12, w12, tabs))
    out = call(
        last_body,
        sds(CELLS, NG),
        (r0, r12, *back_g, *back_f),
        [VMEM((400, CELLS), F32), VMEM((NG, CELLS), F32), VMEM((NG, CELLS), F32)],
        flops=6 * 2 * 400 * NG * CELLS,
        nbytes=6 << 20,
        name="last",
    )
    return out.reshape(48, 24, NG)


def solution(mesh):
    placed = (
        P(("px", "py"), None),
        P(("px", "py"), None),
        P(("px", "py")),
        P(("px", "py"), None),
        P("px", "py", None),
    )
    return jax.shard_map(
        on_device, mesh=mesh, in_specs=placed, out_specs=P("px", "py", None), check_vma=False
    )
```

time: 472 us -> 175 us (0.37); the launches traced: 463 us -> 174 us
  matrix products: 172 us -> 0 us
  local copies, waits for them, and re-layouts: 78.9 us -> 7.73 us
  waiting for transfers between devices: 72.9 us -> 7.55 us
  Pallas kernels: 0 us -> 53.2 us
  other arithmetic: 52 us -> 21.2 us
  blocking collectives: 68.1 us -> 39 us
  starting transfers between devices: 18.6 us -> 39 us
  between operations: 0.75 us -> 6.74 us
    dot_general x18 -> x0, matrix products: 172 us -> none  [product(): return jnp.einsum(form, left, right, precision=lax.Precision.HIGHEST)]
    all_to_all x3 -> x4, waiting for transfers between devices: 72.9 us -> 7.55 us  [the longest x3 4.81 us: exchange(): lax.all_to_all(a, ('px', 'py'), split_axis=0, concat_axis=0, tiled=True)]
    pallas_call x0 -> x6, Pallas kernels: none -> 53.2 us  [call(): pl.pallas_call(body, out_shape=out_shape, in_specs=[pl.BlockSpec(memory_s...]
    scatter-add x1 -> x0, other arithmetic: 43.6 us -> none  [paint(): return empty.at[cell_rows.reshape(-1)].add(weights.reshape(-1))]
    reshape x7 -> x1, local copies, waits for them, and re-layouts: 44.8 us -> 1.34 us  [on_device(): halo_counts.reshape(32, 1)]
    all_to_all x1, blocking collectives: 68.1 us -> 39 us  [exchange(): lax.all_to_all(a, ('px', 'py'), split_axis=0, concat_axis=0, tiled=True)]
    all_to_all x3 -> x4, starting transfers between devices: 18.6 us -> 39 us  [the longest x3 29.6 us: exchange(): lax.all_to_all(a, ('px', 'py'), split_axis=0, concat_axis=0, tiled=True)]
    mul x4 -> x1, other arithmetic: 0.03 us -> 9.07 us  [window(): return top_hat(signed(kx), signed(ky), signed(k)) * scale]
  transfers between devices with their start and end apart: 3 -> 4, of which waited for: 3 -> 3; matrix products, arithmetic and copies ran while one was open for 0% -> 14% of each run, Pallas kernels for 0% -> 25%
where the time goes in v1:
time: 175 us; the launch traced here: 174 us
  Pallas kernels  53.2 us (30%)
  starting transfers between devices  39 us (22%)
  blocking collectives  39 us (22%)
  other arithmetic  21.2 us (12%)
  local copies, waits for them, and re-layouts  7.73 us (4%)
  waiting for transfers between devices  7.55 us (4%)
  between operations  6.74 us (4%)
    pallas_call x6, Pallas kernels, call(): pl.pallas_call(body, out_shape=out_shape, in_specs=[pl.BlockSpec(memory_s...  53.2 us
    all_to_all x1, blocking collectives, exchange(): lax.all_to_all(a, ('px', 'py'), split_axis=0, concat_axis=0, tiled=True)  39 us
    all_to_all x3, starting transfers between devices, exchange(): lax.all_to_all(a, ('px', 'py'), split_axis=0, concat_axis=0, tiled=True)  29.6 us
    all_to_all x1, starting transfers between devices, on_device(): got = lax.all_to_all(send, 'py', split_axis=0, concat_axis=0, tiled=True)  9.45 us
    mul x1, other arithmetic, window(): return top_hat(signed(kx), signed(ky), signed(k)) * scale  9.07 us
    neg x1, other arithmetic, twiddles(): return (jnp.cos(one), -jnp.sin(one), jnp.cos(two), -jnp.sin(two))  8.59 us
    all_to_all x3, waiting for transfers between devices, exchange(): lax.all_to_all(a, ('px', 'py'), split_axis=0, concat_axis=0, tiled=True)  4.81 us
    unnamed x11, local copies, waits for them, and re-layouts  3.78 us
  transfers between devices with their start and end apart: 4, of which 3 were waited for; matrix products, arithmetic and copies ran while one was open for 14% of the time, Pallas kernels for 25%

profile of v1, /device:TPU:1, one launch (start us, length us, event | category | flops | bytes accessed | tf_op | source)
XLA Modules:
  0.0 174.4 jit_solution(18044930123447723247)
XLA Ops:
  0.0 1.3 copy.29.count_ref
  1.3 1.3 copy.30.own_col
  2.7 1.7 prep.1
  4.3 9.4 %all-to-all-start.2 = ((f32[16,8,128]{2,1,0:T(8,128)}), f32[16,8,128]{2,1,0:T(8,128)S(1)}, u32[]{:S(2)}, u32[]{:S(2)}) async-start(f32[16,8,128]{2,1,0:T(8,128)} %prep.1), calls=%async_computation.2 | async-start | bytes 131072 | tf_op jit(solution)/shard_map/all_to_all | solution.py:384
  13.8 4.6 %density.1 = (f32[128,1,2304]{2,1,0:T(1,128)}, f32[144,1152]{1,0:T(8,128)}) custom-call(f32[1152,384]{1,0:T(8,128)} %bitcast.20, bf16[256,384]{1,0:T(8,128)(2,1)} %constant.309.clone.t0h, bf16[256,384]{1,0:T(8,128)(2,1)} %constant.310.clone.t0l, bf16[144,384]{1,0:T(8,128)(2,1)} %constant.311.clone.t1h, bf16[144,384]{1,0:T(8,128)(2,1)} %constant.312.clone.t1l), custom_call_target="tpu_custom_call" | custom-call | flops 1061683200 | bytes 4194304 | tf_op jit(solution)/shard_map/density/pallas_call | solution.py:142
  18.4 2.7 %all-to-all-done.2 = f32[16,8,128]{2,1,0:T(8,128)S(1)} async-done(((f32[16,8,128]{2,1,0:T(8,128)}), f32[16,8,128]{2,1,0:T(8,128)S(1)}, u32[]{:S(2)}, u32[]{:S(2)}) %all-to-all-start.2) | async-done | bytes 65568 | tf_op jit(solution)/shard_map/all_to_all | solution.py:384
  21.1 6.5 %all-to-all-start = ((f32[128,1,2304]{2,1,0:T(1,128)}), f32[128,1,2304]{2,1,0:T(1,128)S(1)}, u32[]{:S(2)}, u32[]{:S(2)}) async-start(f32[128,1,2304]{2,1,0:T(1,128)} %get-tuple-element.7), calls=%async_computation | async-start | bytes 2359296 | tf_op jit(solution)/shard_map/all_to_all | solution.py:345
  27.7 0.3 fusion.80
  28.0 0.7 reduce_sum.12.cnt
  28.7 0.6 slice.8
  29.3 0.1 remainder_compare_fusion
  29.4 0.7 fusion.63.idx
  30.1 17.0 %paint.1 = f32[128,1,4608]{2,1,0:T(1,128)} custom-call(s32[64]{0:T(128)} %reduce_sum.12.cnt, s32[64,128]{1,0:T(8,128)} %fusion.63.idx, f32[64,128]{1,0:T(8,128)} %bitcast.15, bf16[256,384]{1,0:T(8,128)(2,1)} %constant.309.clone.t0h, bf16[256,384]{1,0:T(8,128)(2,1)} %constant.310.clone.t0l, bf16[144,384]{1,0:T(8,128)(2,1)} %constant.313.clone.t1h, ...), custom_call_target="tpu_custom_call" | custom-call | flops 3185049600 | bytes 4194304 | tf_op jit(solution)/shard_map/paint/pallas_call | solution.py:142
  47.1 0.0 copy-start.4
  47.1 0.0 copy-start.3
  47.1 1.0 all-to-all-done.x
  48.1 0.0 copy-start.1
  48.1 1.0 copy-done.1
  49.1 13.3 %all-to-all-start.3 = ((f32[128,1,4608]{2,1,0:T(1,128)}), f32[128,1,4608]{2,1,0:T(1,128)S(1)}, u32[]{:S(2)}, u32[]{:S(2)}) async-start(f32[128,1,4608]{2,1,0:T(1,128)} %paint.1), calls=%async_computation.3 | async-start | bytes 4718592 | tf_op jit(solution)/shard_map/all_to_all | solution.py:345
  62.4 0.0 copy-done.4
  62.5 0.7 dynamic_slice.10
  65.0 0.0 copy-done.3
  65.0 0.7 dynamic_slice.9
  70.5 8.6 %sine_negate_fusion = (f32[1152,128]{1,0:T(8,128)}, f32[1152,128]{1,0:T(8,128)}, f32[1152,128]{1,0:T(8,128)}, f32[1152,128]{1,0:T(8,128)}) fusion(s32[128]{0:T(128)S(1)} %get-tuple-element.30, s32[128]{0:T(128)S(1)} %get-tuple-element.31, pred[128]{0:T(512)(128)(4,1)S(1)} %get-tuple-element.27, s32[1152]{0:T(1024)S(1)} %get-tuple-element.21, ...), kind=kLoop, calls=%fused_computation.85 | loop fusion | flops 9584640 | bytes 2382336 | tf_op jit(solution)/shard_map/neg | solution.py:117
  79.1 9.1 %fusion.12 = (f32[1,1152,128]{2,1,0:T(8,128)}, f32[1,1152,128]{2,1,0:T(8,128)}) fusion(f32[]{:T(128)S(6)} %div.298, f32[]{:T(128)S(6)} %mul.489, s32[128]{0:T(128)S(1)} %get-tuple-element.30, s32[128]{0:T(128)S(1)} %get-tuple-element.31, pred[128]{0:T(512)(128)(4,1)S(1)} %get-tuple-element.27, s32[128]{0:T(128)S(1)} %get-tuple-element.29, ...), kind=kLoop, calls=%fused_computation.49 | loop fusion | flops 11501568 | bytes 1202704 | tf_op jit(solution)/shard_map/mul | solution.py:136
  88.1 8.5 %planes.2 = f32[128,1,2304]{2,1,0:T(1,128)} custom-call(f32[128,1,2304]{2,1,0:T(1,128)} %copy-done.1, f32[1,1152,128]{2,1,0:T(8,128)} %get-tuple-element.16.w, bf16[256,256]{1,0:T(8,128)(2,1)} %constant.319.clone.ah, bf16[256,256]{1,0:T(8,128)(2,1)} %constant.320.clone.al, bf16[256,256]{1,0:T(8,128)(2,1)} %constant.321.clone.bh, ...), custom_call_target="tpu_custom_call" | custom-call | flops 1811939328 | bytes 2359296 | tf_op jit(solution)/shard_map/planes/pallas_call | solution.py:142
  96.7 0.0 all-to-all-done.3.x
  96.7 0.0 copy-start
  96.7 1.4 copy-done
  98.1 9.8 %all-to-all-start.1 = ((f32[128,1,2304]{2,1,0:T(1,128)}), f32[128,1,2304]{2,1,0:T(1,128)S(1)}, u32[]{:S(2)}, u32[]{:S(2)}) async-start(f32[128,1,2304]{2,1,0:T(1,128)} %planes.2), calls=%async_computation.1 | async-start | bytes 2359296 | tf_op jit(solution)/shard_map/all_to_all | solution.py:345
  107.9 2.3 %pad_maximum_fusion.w = f32[2,1152,128]{2,1,0:T(8,128)} fusion(f32[1,1152,128]{2,1,0:T(8,128)} %get-tuple-element.16.w, f32[1,1152,128]{2,1,0:T(8,128)} %get-tuple-element.15), kind=kLoop, calls=%fused_computation.10 | loop fusion | flops 294912 | bytes 2359296 | tf_op jit(solution)/shard_map/stack | solution.py:415
  110.2 14.4 %planes.3 = f32[128,1,4608]{2,1,0:T(1,128)} custom-call(f32[128,1,4608]{2,1,0:T(1,128)} %copy-done, f32[2,1152,128]{2,1,0:T(8,128)} %pad_maximum_fusion.w, bf16[256,256]{1,0:T(8,128)(2,1)} %constant.319.clone.ah, bf16[256,256]{1,0:T(8,128)(2,1)} %constant.320.clone.al, bf16[256,256]{1,0:T(8,128)(2,1)} %constant.321.clone.bh, ...), custom_call_target="tpu_custom_call" | custom-call | flops 3623878656 | bytes 4718592 | tf_op jit(solution)/shard_map/planes/pallas_call | solution.py:142
  124.6 3.8 %all-to-all-done.1.r0 = f32[128,1,2304]{2,1,0:T(1,128)S(1)} async-done(((f32[128,1,2304]{2,1,0:T(1,128)}), f32[128,1,2304]{2,1,0:T(1,128)S(1)}, u32[]{:S(2)}, u32[]{:S(2)}) %all-to-all-start.1) | async-done | bytes 1179680 | tf_op jit(solution)/shard_map/all_to_all | solution.py:345
  128.3 0.0 copy-start.2
  128.3 39.0 %all_to_all.25.r12 = f32[128,1,4608]{2,1,0:T(1,128)} all-to-all(f32[128,1,4608]{2,1,0:T(1,128)} %planes.3), channel_id=1, replica_groups=mesh['px'=8,'py'=16] {'px','py'}, dimensions={0} | all-to-all | bytes 4718592 | tf_op jit(solution)/shard_map/all_to_all | solution.py:345
  167.3 0.0 copy-done.2
  167.3 7.1 %last.1 = f32[1152,384]{1,0:T(8,128)} custom-call(f32[128,1,2304]{2,1,0:T(1,128)} %copy-done.2, f32[128,1,4608]{2,1,0:T(1,128)} %all_to_all.25.r12, bf16[384,400]{1,0:T(8,128)(2,1)} %constant.315.clone.gth, bf16[384,400]{1,0:T(8,128)(2,1)} %constant.316.clone.gtl, bf16[384,400]{1,0:T(8,128)(2,1)} %constant.317.clone.fth, bf16[384,400]{1,0:T(8,128)(2,1)} %constant.318.clone.ftl), custom_call_target="tpu_custom_call" | custom-call | flops 2123366400 | bytes 6291456 | tf_op jit(solution)/shard_map/last/pallas_call | solution.py:142
  (6 shorter events, 0.0 us)
Async XLA Ops:
  4.3 16.8 %all-to-all-start.2 = ((f32[16,8,128]{2,1,0:T(8,128)}), f32[16,8,128]{2,1,0:T(8,128)S(1)}, u32[]{:S(2)}, u32[]{:S(2)}) async-start(f32[16,8,128]{2,1,0:T(8,128)} %prep.1), calls=%async_computation.2 | async-start | bytes 131072 | tf_op jit(solution)/shard_map/all_to_all | solution.py:384
  21.1 27.0 %all-to-all-start = ((f32[128,1,2304]{2,1,0:T(1,128)}), f32[128,1,2304]{2,1,0:T(1,128)S(1)}, u32[]{:S(2)}, u32[]{:S(2)}) async-start(f32[128,1,2304]{2,1,0:T(1,128)} %get-tuple-element.7), calls=%async_computation | async-start | bytes 2359296 | tf_op jit(solution)/shard_map/all_to_all | solution.py:345
  47.1 15.4 %copy-start.4 = (s32[128]{0:T(128)S(1)}, s32[128]{0:T(128)}, u32[]{:S(2)}) copy-start(s32[128]{0:T(128)} %constant.328.clone) | copy-start | bytes 1540
  47.1 17.9 %copy-start.3 = (s32[128]{0:T(128)S(1)}, s32[128]{0:T(128)}, u32[]{:S(2)}) copy-start(s32[128]{0:T(128)} %constant.327.clone) | copy-start | bytes 1540
  48.1 1.0 copy-start.1
  49.1 47.5 %all-to-all-start.3 = ((f32[128,1,4608]{2,1,0:T(1,128)}), f32[128,1,4608]{2,1,0:T(1,128)S(1)}, u32[]{:S(2)}, u32[]{:S(2)}) async-start(f32[128,1,4608]{2,1,0:T(1,128)} %paint.1), calls=%async_computation.3 | async-start | bytes 4718592 | tf_op jit(solution)/shard_map/all_to_all | solution.py:345
  96.7 1.4 copy-start
  98.1 30.2 %all-to-all-start.1 = ((f32[128,1,2304]{2,1,0:T(1,128)}), f32[128,1,2304]{2,1,0:T(1,128)S(1)}, u32[]{:S(2)}, u32[]{:S(2)}) async-start(f32[128,1,2304]{2,1,0:T(1,128)} %planes.2), calls=%async_computation.1 | async-start | bytes 2359296 | tf_op jit(solution)/shard_map/all_to_all | solution.py:345
  128.3 39.0 %copy-start.2 = (f32[128,1,2304]{2,1,0:T(1,128)}, f32[128,1,2304]{2,1,0:T(1,128)S(1)}, u32[]{:S(2)}) copy-start(f32[128,1,2304]{2,1,0:T(1,128)S(1)} %all-to-all-done.1.r0) | copy-start | bytes 3538948

commit v2 on v1

--- a/solution.py
+++ b/solution.py
@@ -102,19 +102,13 @@
     return np.block([[re, im], [-im, re]])
 
 
-def freq_parts():
-    row = lax.broadcasted_iota(jnp.int32, (CELLS, 128), 0)
-    lane = lax.broadcasted_iota(jnp.int32, (CELLS, 128), 1)
+def twiddles():
+    row, lane = np.arange(CELLS)[:, None], np.arange(128)[None]
     m, s = row // 128, row % 128
-    return s // 16, s % 16, m // 3, m % 3, lane // 8, lane % 8
-
-
-def twiddles():
-    ax, ay, bx, by, cx, cy = freq_parts()
-    w = 2.0 * jnp.pi / NG
-    one = ((ax * bx * 16 + ay * by * 8) % NG).astype(F32) * w
-    two = ((cx * (ax + 8 * bx) + cy * (ay + 16 * by)) % NG).astype(F32) * w
-    return jnp.cos(one), -jnp.sin(one), jnp.cos(two), -jnp.sin(two)
+    ax, ay, bx, by, cx, cy = s // 16, s % 16, m // 3, m % 3, lane // 8, lane % 8
+    one = (ax * bx * 16 + ay * by * 8 + 0 * lane) * (2 * np.pi / NG)
+    two = (cx * (ax + 8 * bx) + cy * (ay + 16 * by)) * (2 * np.pi / NG)
+    return np.stack([np.cos(one), -np.sin(one), np.cos(two), -np.sin(two)]).astype(np.float32)
 
 
 def signed(k):
@@ -126,14 +120,6 @@
     safe = jnp.where(radial > 0, radial, 1.0)
     value = 3.0 * (jnp.sin(safe) - safe * jnp.cos(safe)) / (safe * safe * safe)
     return jnp.where(radial > 0, value, 1.0)
-
-
-def window(me, kz):
-    ax, ay, bx, by, cx, cy = freq_parts()
-    kx, ky = ax + 8 * bx + 24 * cx, ay + 16 * by + 48 * cy
-    k = jnp.asarray(kz, jnp.int32)[me]
-    scale = jnp.where((k == 0) | (k == NG // 2), 1.0, 2.0) / float(NG) ** 3
-    return top_hat(signed(kx), signed(ky), signed(k)) * scale
 
 
 def call(body, out_shape, args, scratch, spaces=None, flops=0, nbytes=0, name=None, **params):
@@ -151,18 +137,30 @@
     )(*args)
 
 
-def prep_body(ph_ref, cell_ref, count_ref, own_col, own_row, out_ref):
+def prep_body(ph_ref, cell_ref, count_row, own_row, out_ref):
     lane = lax.broadcasted_iota(jnp.int32, (32, SLOTS), 1)
-    live = lane < count_ref[...]
+    first = lax.broadcasted_iota(jnp.int32, (32, 32), 0)
+    second = lax.broadcasted_iota(jnp.int32, (32, 32), 1)
+
+    def column(row):
+        spread = jnp.where(first == second, row.astype(F32), 0.0)
+        return jnp.sum(spread, axis=1, keepdims=True).astype(jnp.int32)
+
+    live = lane < column(count_row[...])
     w = jnp.where(live, ph_ref[...], 0.0)
-    cells = jnp.where(live, cell_ref[...], 0).astype(F32)
-    before = lax.broadcasted_iota(jnp.int32, (32, 32), 0) < lax.broadcasted_iota(jnp.int32, (32, 32), 1)
-    same = (own_col[...] == own_row[...]) & before
+    cell = jnp.where(live, cell_ref[...], 0)
+    column_of = cell // NG
+    gz = cell - column_of * NG
+    gx = column_of // 24
+    gy = column_of - gx * 24
+    chunk = (gz >> 7) * 9 + (gx >> 4) * 3 + (gy >> 3)
+    spot = ((chunk * 128 + (gx & 15) * 8 + (gy & 7)) * 128 + (gz & 127)).astype(F32)
+    same = (column(own_row[...]) == own_row[...]) & (first < second)
     rank = jnp.sum(jnp.where(same, 1.0, 0.0), axis=0, keepdims=True).astype(jnp.int32)
     place = own_row[...] * (2 * CAP) + rank
     rows = lax.broadcasted_iota(jnp.int32, (DEV, 32), 0)
     total = jnp.zeros((DEV, SLOTS), F32)
-    for values, shift in ((w, 0), (cells, CAP)):
+    for values, shift in ((w, 0), (spot, CAP)):
         hot = jnp.where(rows == place + shift, 1.0, 0.0).astype(BF16)
         hi = values.astype(BF16)
         rest = values - hi.astype(F32)
@@ -189,7 +187,7 @@
 UNROLL = 8
 
 
-def paint_body(cnt, idx, ph, t0h, t0l, t1h, t1l, y1, x12, b0, b1, b2, b3, fh, fl):
+def paint_body(got, t0h, t0l, t1h, t1l, y1, x12, b0, b1, b2, b3, fh, fl):
     bufs = (b0, b1, b2, b3)
     zero = jnp.zeros((128, 128), F32)
 
@@ -203,17 +201,23 @@
     lane = lax.broadcasted_iota(jnp.int32, (1, 128), 1)
 
     def one_row(r, carry):
-        def step(jb, inner):
+        src, slot = r >> 2, r & 3
+
+        def more(jb):
+            return (jb < SLOTS // UNROLL) & (got[src, slot, jnp.minimum(jb * UNROLL, SLOTS - 1)] > 0.0)
+
+        def step(jb):
             for u in range(UNROLL):
                 j = jb * UNROLL + u
-                at = idx[r, j]
+                at = got[src, CAP + slot, j].astype(jnp.int32)
                 b = bufs[u % BUFS]
                 row = lax.shift_right_logical(at, 7)
                 here = lane == lax.bitwise_and(at, 127)
-                b[pl.ds(row, 1), :] = b[pl.ds(row, 1), :] + jnp.where(here, ph[r, j], 0.0)
-            return inner
-
-        return lax.fori_loop(0, (cnt[r] + UNROLL - 1) // UNROLL, step, carry)
+                b[pl.ds(row, 1), :] = b[pl.ds(row, 1), :] + jnp.where(here, got[src, slot, j], 0.0)
+            return jb + 1
+
+        lax.while_loop(more, step, 0)
+        return carry
 
     lax.fori_loop(0, 16 * CAP, one_row, 0)
     for m in range(9):
@@ -260,71 +264,178 @@
 
 
 RB = 16
-
-
-def planes_body(n, x, w, ah, al, bh, bl, ch, cl, dh, dl, c1, s1, c2, s2, y, wide, tall, uh, ul, vh, vl):
-    for p in range(n):
-        base = p * PLANE
+MESH = pl.DeviceIdType.MESH
+
+
+def coords():
+    px, py = lax.axis_index("px"), lax.axis_index("py")
+    return px & 3, ((py >> 1) & 1) * 2 + (px >> 2), py >> 2, py & 1
+
+
+def partner(t):
+    x, y, z, core = coords()
+    u = (t * 101) & 127
+    sign = 1 - 2 * core
+    x2 = (x + sign * ((u >> 1) & 3)) & 3
+    y2 = (y + sign * ((u >> 3) & 3)) & 3
+    z2 = (z + sign * ((u >> 5) & 3)) & 3
+    return (y2 & 1) * 4 + x2, z2 * 4 + (y2 >> 1) * 2 + ((core + u) & 1)
+
+
+def everyone(body):
+    def step(t, carry):
+        body(*partner(t))
+        return carry
+
+    lax.fori_loop(1, DEV, step, 0)
+
+
+def fill_window(me, win):
+    second = jnp.where(me < 63, 129 + me, jnp.where(me == 63, 0, jnp.where(me == 64, NG // 2, 64 + me)))
+    lane = lax.broadcasted_iota(jnp.int32, (RB, 128), 1)
+    sub = lax.broadcasted_iota(jnp.int32, (RB, 128), 0)
+    for which, k in ((0, me + 1), (1, second)):
+        scale = jnp.where((k == 0) | (k == NG // 2), 1.0, 2.0) / float(NG) ** 3
+        fz = signed(k)
+
+        def step(i, carry):
+            m, r = i // (DEV // RB), i % (DEV // RB)
+            s = sub + r * RB
+            bx = m // 3
+            kx = (s >> 4) + 8 * bx + 24 * (lane >> 3)
+            ky = (s & 15) + 16 * (m - 3 * bx) + 48 * (lane & 7)
+            value = top_hat(signed(kx), signed(ky), fz) * scale
+            win[which, pl.ds(pl.multiple_of(i * RB, RB), RB), :] = value
+            return carry
+
+        lax.fori_loop(0, CELLS // RB, step, 0)
+
+
+def planes_body(
+    x0, x12, tw_hbm, ah, al, bh, bl, ch, cl, dh, dl, out,
+    xs, ys, win, tw, wide, tall, uh, ul, vh, vl, sx, rx, sy, ry, own, sl,
+):
+    px, py = lax.axis_index("px"), lax.axis_index("py")
+    me = px * 16 + py
+    loads = [
+        pltpu.make_async_copy(x0, xs.at[0], sl.at[0]),
+        pltpu.make_async_copy(tw_hbm, tw, sl.at[1]),
+    ]
+    for q in range(2):
+        mine = x12.at[me, :, pl.ds(q * PLANE, PLANE)]
+        loads.append(pltpu.make_async_copy(mine, xs.at[q + 1, me], sl.at[2 + q]))
+    for c in loads:
+        c.start()
+    barrier = pltpu.get_barrier_semaphore()
+    everyone(lambda a, b: pl.semaphore_signal(barrier, inc=1, device_id=(a, b), device_id_type=MESH))
+    pl.semaphore_wait(barrier, DEV - 1)
+    for q in range(2):
+        everyone(
+            lambda a, b: pltpu.make_async_remote_copy(
+                src_ref=x12.at[a * 16 + b, :, pl.ds(q * PLANE, PLANE)],
+                dst_ref=xs.at[q + 1, me],
+                send_sem=sx.at[q],
+                recv_sem=rx.at[q],
+                device_id=(a, b),
+                device_id_type=MESH,
+            ).start()
+        )
+    fill_window(me, win)
+    for c in loads:
+        c.wait()
+
+    def one_plane(p, carry):
+        @pl.when(p > 0)
+        def _():
+            part = xs.at[p, pl.ds(0, DEV - 1)]
+            pltpu.make_async_copy(part, part, rx.at[p - 1]).wait()
+
         for c in range(2):
-            wide[c * DEV : (c + 1) * DEV, :] = x[:, 0, base + c * CELLS : base + (c + 1) * CELLS]
+            wide[c * DEV : (c + 1) * DEV, :] = xs[p, :, 0, c * CELLS : (c + 1) * CELLS]
         hi, lo = cut(wide[...])
         wide[...] = mm3(ah[...], al[...], hi, lo)
 
-        def forward(i, carry):
+        def forward(i, inner):
             r = pl.multiple_of(i * RB, RB)
             v = []
             for m in range(9):
                 cols = slice(m * 128, (m + 1) * 128)
                 t = pl.ds(m * 128 + r, RB)
                 u = (wide[pl.ds(r, RB), cols], wide[pl.ds(DEV + r, RB), cols])
-                v.append(turn(u, c1[t, :], s1[t, :]))
+                v.append(turn(u, tw[0, t, :], tw[1, t, :]))
             for m, u in enumerate(nine(v, False)):
                 t = pl.ds(m * 128 + r, RB)
-                for c, part in enumerate(turn(u, c2[t, :], s2[t, :])):
+                for c, part in enumerate(turn(u, tw[2, t, :], tw[3, t, :])):
                     hi, lo = cut(part)
                     uh[t, c * 128 : (c + 1) * 128] = hi
                     ul[t, c * 128 : (c + 1) * 128] = lo
-            return carry
+            return inner
 
         lax.fori_loop(0, DEV // RB, forward, 0)
         mid = mm3(uh[...], ul[...], ch[...], cl[...])
-        win = w[p]
+        this = win[p & 1]
         for c in range(2):
-            hi, lo = cut(mid[:, c * 128 : (c + 1) * 128] * win)
+            hi, lo = cut(mid[:, c * 128 : (c + 1) * 128] * this)
             uh[:, c * 128 : (c + 1) * 128] = hi
             ul[:, c * 128 : (c + 1) * 128] = lo
         tall[...] = mm3(uh[...], ul[...], dh[...], dl[...])
 
-        def backward(i, carry):
+        def backward(i, inner):
             r = pl.multiple_of(i * RB, RB)
             v = []
             for m in range(9):
                 t = pl.ds(m * 128 + r, RB)
-                v.append(turn((tall[t, :128], tall[t, 128:]), c2[t, :], -s2[t, :]))
+                v.append(turn((tall[t, :128], tall[t, 128:]), tw[2, t, :], -tw[3, t, :]))
             for m, u in enumerate(nine(v, True)):
                 t = pl.ds(m * 128 + r, RB)
                 cols = slice(m * 128, (m + 1) * 128)
-                for c, part in enumerate(turn(u, c1[t, :], -s1[t, :])):
+                for c, part in enumerate(turn(u, tw[0, t, :], -tw[1, t, :])):
                     hi, lo = cut(part)
                     vh[pl.ds(c * DEV + r, RB), cols] = hi
                     vl[pl.ds(c * DEV + r, RB), cols] = lo
-            return carry
+            return inner
 
         lax.fori_loop(0, DEV // RB, backward, 0)
         back = mm3(bh[...], bl[...], vh[...], vl[...])
         for c in range(2):
-            y[:, 0, base + c * CELLS : base + (c + 1) * CELLS] = back[c * DEV : (c + 1) * DEV]
-
-
-def last_body(r0, r12, gth, gtl, fth, ftl, out, stack, ga, fa):
+            ys[p, :, 0, c * CELLS : (c + 1) * CELLS] = back[c * DEV : (c + 1) * DEV]
+        mine = pltpu.make_async_copy(ys.at[p, me], out.at[p, me], own)
+        mine.start()
+        mine.wait()
+        everyone(
+            lambda a, b: pltpu.make_async_remote_copy(
+                src_ref=ys.at[p, a * 16 + b],
+                dst_ref=out.at[p, me],
+                send_sem=sy.at[p],
+                recv_sem=ry.at[p],
+                device_id=(a, b),
+                device_id_type=MESH,
+            ).start()
+        )
+        return carry
+
+    lax.fori_loop(0, 3, one_plane, 0)
+    for q in range(2):
+        part = x12.at[pl.ds(0, DEV - 1), :, pl.ds(q * PLANE, PLANE)]
+        pltpu.make_async_copy(part, part, sx.at[q]).wait()
+    for p in range(3):
+        part = ys.at[p, pl.ds(0, DEV - 1)]
+        pltpu.make_async_copy(part, part, sy.at[p]).wait()
+        part = out.at[p, pl.ds(0, DEV - 1)]
+        pltpu.make_async_copy(part, part, ry.at[p]).wait()
+
+
+def last_body(r, gth, gtl, fth, ftl, out, stack, ga, fa):
     for c in range(2):
-        stack[c * DEV : (c + 1) * DEV, :] = r0[:, 0, c * CELLS : (c + 1) * CELLS]
-        stack[2 * DEV + c * HEAD : 2 * DEV + (c + 1) * HEAD, :] = r12[:HEAD, 0, c * CELLS : (c + 1) * CELLS]
+        cols = slice(c * CELLS, (c + 1) * CELLS)
+        stack[c * DEV : (c + 1) * DEV, :] = r[0, :, 0, cols]
+        stack[2 * DEV + c * HEAD : 2 * DEV + (c + 1) * HEAD, :] = r[1, :HEAD, 0, cols]
     hi, lo = cut(stack[...])
     ga[...] = mm3(gth[...], gtl[...], hi, lo)
     for c in range(2):
-        stack[c * DEV : (c + 1) * DEV, :] = r12[:, 0, PLANE + c * CELLS : PLANE + (c + 1) * CELLS]
-        stack[2 * DEV + c * HEAD : 2 * DEV + (c + 1) * HEAD, :] = r12[TAIL:, 0, c * CELLS : (c + 1) * CELLS]
+        cols = slice(c * CELLS, (c + 1) * CELLS)
+        stack[c * DEV : (c + 1) * DEV, :] = r[2, :, 0, cols]
+        stack[2 * DEV + c * HEAD : 2 * DEV + (c + 1) * HEAD, :] = r[1, TAIL:, 0, cols]
     hi, lo = cut(stack[...])
     fa[...] = mm3(fth[...], ftl[...], hi, lo)
     for m in range(9):
@@ -345,19 +456,36 @@
     return lax.all_to_all(a, ("px", "py"), split_axis=0, concat_axis=0, tiled=True)
 
 
-def planes(x, w, tabs):
-    n = w.shape[0]
-    return call(
-        functools.partial(planes_body, n),
-        sds(DEV, 1, n * PLANE),
-        (x, w, *tabs),
-        [VMEM((256, CELLS), F32), VMEM((CELLS, 256), F32)]
-        + [VMEM((CELLS, 256), BF16)] * 2
-        + [VMEM((256, CELLS), BF16)] * 2,
-        flops=n * 4 * 3 * 2 * 256 * 256 * CELLS,
-        nbytes=n * PLANE * DEV * 8,
+def planes(x0, x12, tw, mats):
+    dma = pltpu.SemaphoreType.DMA
+    plane = (DEV, 1, PLANE)
+    return pl.pallas_call(
+        planes_body,
+        out_shape=sds(3, *plane),
+        in_specs=[pl.BlockSpec(memory_space=pl.ANY)] * 3 + [pl.BlockSpec(memory_space=VMEM)] * 8,
+        out_specs=pl.BlockSpec(memory_space=pl.ANY),
+        scratch_shapes=[
+            VMEM((3, *plane), F32),
+            VMEM((3, *plane), F32),
+            VMEM((2, CELLS, 128), F32),
+            VMEM((4, CELLS, 128), F32),
+            VMEM((256, CELLS), F32),
+            VMEM((CELLS, 256), F32),
+            VMEM((CELLS, 256), BF16),
+            VMEM((CELLS, 256), BF16),
+            VMEM((256, CELLS), BF16),
+            VMEM((256, CELLS), BF16),
+            dma((2,)),
+            dma((2,)),
+            dma((3,)),
+            dma((3,)),
+            dma,
+            dma((4,)),
+        ],
+        compiler_params=pltpu.CompilerParams(vmem_limit_bytes=LIMIT, collective_id=1, has_side_effects=True),
+        cost_estimate=pl.CostEstimate(flops=36 << 30, bytes_accessed=8 << 20, transcendentals=0),
         name="planes",
-    )
+    )(x0, x12, tw, *mats)
 
 
 def on_device(photons, halo_cells, halo_counts, owners, density):
@@ -370,12 +498,11 @@
     mats = []
     for m in (row_matrix(1), row_matrix(-1), lane_matrix(1), lane_matrix(-1)):
         mats += [jnp.asarray(t) for t in cut_np(m)]
-    me = lax.axis_index(("px", "py"))
 
     send = call(
         prep_body,
         sds(16, 2 * CAP, SLOTS),
-        (photons, halo_cells, halo_counts.reshape(32, 1), owners, owners.reshape(1, 32)),
+        (photons, halo_cells, halo_counts.reshape(1, 32), owners.reshape(1, 32)),
         [],
         flops=1 << 20,
         nbytes=1 << 17,
@@ -392,32 +519,21 @@
         name="density",
     )
     x0 = exchange(x0)
-    ph = got[:, :CAP].reshape(16 * CAP, SLOTS)
-    cell = got[:, CAP:].reshape(16 * CAP, SLOTS).astype(jnp.int32)
-    cnt = jnp.sum((ph > 0).astype(jnp.int32), axis=1)
-    gx, gy, gz = cell // (24 * NG), cell // NG % 24, cell % NG
-    chunk = gx // 16 * 3 + gy // 8
-    idx = (((gz // 128) * 9 + chunk) * 128 + gx % 16 * 8 + gy % 8) * 128 + gz % 128
     x12 = call(
         paint_body,
         sds(DEV, 1, 2 * PLANE),
-        (cnt, idx, ph, *t0, *t1f, y1),
+        (got, *t0, *t1f, y1),
         [VMEM((3 * CELLS, 128), F32)] * BUFS + [VMEM((CELLS, NG), BF16)] * 2,
-        spaces=[SMEM] * 3 + [VMEM] * 5,
+        spaces=[SMEM] + [VMEM] * 5,
         flops=6 * 400 * NG * CELLS * 3,
         nbytes=4 << 20,
         name="paint",
     )
-    x12 = exchange(x12)
-    tabs = (*mats, *twiddles())
-    r0 = planes(x0, window(me, kz_first())[None], tabs)
-    r0 = exchange(r0)
-    w12 = jnp.stack([window(me, kz_second()), window(me, kz_first())])
-    r12 = exchange(planes(x12, w12, tabs))
+    r = planes(x0, x12, jnp.asarray(twiddles()), mats)
     out = call(
         last_body,
         sds(CELLS, NG),
-        (r0, r12, *back_g, *back_f),
+        (r, *back_g, *back_f),
         [VMEM((400, CELLS), F32), VMEM((NG, CELLS), F32), VMEM((NG, CELLS), F32)],
         flops=6 * 2 * 400 * NG * CELLS,
         nbytes=6 << 20,

time: 175 us -> 150 us (0.86)
  Pallas kernels: 53.2 us -> 129 us
  blocking collectives: 39 us -> 0 us
  starting transfers between devices: 39 us -> 16 us
  other arithmetic: 21.2 us -> 0 us
  local copies, waits for them, and re-layouts: 7.73 us -> 1.02 us
  between operations: 6.74 us -> 0.03 us
  waiting for transfers between devices: 7.55 us -> 3.14 us
    pallas_call x0 -> x1, Pallas kernels: none -> 95.2 us  [planes(): pl.pallas_call(planes_body, out_shape=sds(3, *plane), in_specs=[pl.BlockS...]
    all_to_all x1 -> x0, blocking collectives: 39 us -> none  [exchange(): lax.all_to_all(a, ('px', 'py'), split_axis=0, concat_axis=0, tiled=True)]
    all_to_all x3 -> x1, starting transfers between devices: 29.6 us -> 6.52 us  [exchange(): lax.all_to_all(a, ('px', 'py'), split_axis=0, concat_axis=0, tiled=True)]
    pallas_call x6 -> x4, Pallas kernels: 53.2 us -> 33.4 us  [call(): pl.pallas_call(body, out_shape=out_shape, in_specs=[pl.BlockSpec(memory_s...]
    mul x1 -> x0, other arithmetic: 9.07 us -> none  [window(): return top_hat(signed(kx), signed(ky), signed(k)) * scale]
    neg x1 -> x0, other arithmetic: 8.59 us -> none  [twiddles(): return (jnp.cos(one), -jnp.sin(one), jnp.cos(two), -jnp.sin(two))]
    all_to_all x3 -> x1, waiting for transfers between devices: 4.81 us -> 0.39 us  [exchange(): lax.all_to_all(a, ('px', 'py'), split_axis=0, concat_axis=0, tiled=True)]
    unnamed x11 -> x4, local copies, waits for them, and re-layouts: 3.78 us -> 1.02 us
  transfers between devices with their start and end apart: 4 -> 2, of which waited for: 3 -> 2; matrix products, arithmetic and copies ran while one was open for 14% -> 0% of each run, Pallas kernels for 25% -> 17%
where the time goes in v2:
time: 150 us; the launch traced here: 149 us
  Pallas kernels  129 us (86%)
  starting transfers between devices  16 us (11%)
  waiting for transfers between devices  3.14 us (2%)
    pallas_call x1, Pallas kernels, planes(): pl.pallas_call(planes_body, out_shape=sds(3, *plane), in_specs=[pl.BlockS...  95.2 us
    pallas_call x4, Pallas kernels, call(): pl.pallas_call(body, out_shape=out_shape, in_specs=[pl.BlockSpec(memory_s...  33.4 us
    all_to_all x1, starting transfers between devices, on_device(): got = lax.all_to_all(send, 'py', split_axis=0, concat_axis=0, tiled=True)  9.45 us
    all_to_all x1, starting transfers between devices, exchange(): lax.all_to_all(a, ('px', 'py'), split_axis=0, concat_axis=0, tiled=True)  6.52 us
  transfers between devices with their start and end apart: 2, of which 2 were waited for; matrix products, arithmetic and copies ran while one was open for 0% of the time, Pallas kernels for 17%

profile of v2, /device:TPU:1, one launch (start us, length us, event | category | flops | bytes accessed | tf_op | source)
XLA Modules:
  0.0 148.8 jit_solution(13048214082235241408)
XLA Ops:
  0.0 1.7 %prep.1 = f32[16,8,128]{2,1,0:T(8,128)} custom-call(f32[32,128]{1,0:T(8,128)} %ph_ref.1, s32[32,128]{1,0:T(8,128)} %cell_ref.1, s32[1,32]{1,0:T(1,128)} %bitcast.4, s32[1,32]{1,0:T(1,128)} %bitcast.5), custom_call_target="tpu_custom_call" | custom-call | flops 1048576 | bytes 131072 | tf_op jit(solution)/shard_map/prep/pallas_call | solution.py:128
  1.7 9.4 %all-to-all-start.1 = ((f32[16,8,128]{2,1,0:T(8,128)}), f32[16,8,128]{2,1,0:T(8,128)S(1)}, u32[]{:S(2)}, u32[]{:S(2)}) async-start(f32[16,8,128]{2,1,0:T(8,128)} %prep.1), calls=%async_computation.1 | async-start | bytes 131072 | tf_op jit(solution)/shard_map/all_to_all | solution.py:511
  11.1 4.6 %density.1 = (f32[128,1,2304]{2,1,0:T(1,128)}, f32[144,1152]{1,0:T(8,128)}) custom-call(f32[1152,384]{1,0:T(8,128)} %bitcast.6, bf16[256,384]{1,0:T(8,128)(2,1)} %constant.38.clone.t0h, bf16[256,384]{1,0:T(8,128)(2,1)} %constant.39.clone.t0l, bf16[144,384]{1,0:T(8,128)(2,1)} %constant.40.clone.t1h, bf16[144,384]{1,0:T(8,128)(2,1)} %constant.41.clone.t1l), custom_call_target="tpu_custom_call" | custom-call | flops 1061683200 | bytes 4194304 | tf_op jit(solution)/shard_map/density/pallas_call | solution.py:128
  15.7 2.7 %all-to-all-done.1.got = f32[16,8,128]{2,1,0:T(8,128)S(1)} async-done(((f32[16,8,128]{2,1,0:T(8,128)}), f32[16,8,128]{2,1,0:T(8,128)S(1)}, u32[]{:S(2)}, u32[]{:S(2)}) %all-to-all-start.1) | async-done | bytes 65568 | tf_op jit(solution)/shard_map/all_to_all | solution.py:511
  18.4 0.0 copy-start.1
  18.5 6.5 %all-to-all-start = ((f32[128,1,2304]{2,1,0:T(1,128)}), f32[128,1,2304]{2,1,0:T(1,128)S(1)}, u32[]{:S(2)}, u32[]{:S(2)}) async-start(f32[128,1,2304]{2,1,0:T(1,128)} %get-tuple-element.7), calls=%async_computation | async-start | bytes 2359296 | tf_op jit(solution)/shard_map/all_to_all | solution.py:456
  25.0 0.0 copy-done.1
  25.0 20.1 %paint.1.x12 = f32[128,1,4608]{2,1,0:T(1,128)} custom-call(f32[16,8,128]{2,1,0:T(8,128)} %copy-done.1, bf16[256,384]{1,0:T(8,128)(2,1)} %constant.38.clone.t0h, bf16[256,384]{1,0:T(8,128)(2,1)} %constant.39.clone.t0l, bf16[144,384]{1,0:T(8,128)(2,1)} %constant.42.clone.t1h, bf16[144,384]{1,0:T(8,128)(2,1)} %constant.43.clone.t1l, ...), custom_call_target="tpu_custom_call" | custom-call | flops 3185049600 | bytes 4194304 | tf_op jit(solution)/shard_map/paint/pallas_call | solution.py:128
  45.0 0.4 all-to-all-done.x0
  45.4 0.0 copy-start
  45.4 1.0 copy-done
  46.5 95.2 %planes.1.r = f32[3,128,1,2304]{3,2,1,0:T(1,128)} custom-call(f32[128,1,2304]{2,1,0:T(1,128)} %copy-done, f32[128,1,4608]{2,1,0:T(1,128)} %paint.1.x12, f32[4,1152,128]{2,1,0:T(8,128)} %constant.56.clone.tw_hbm, bf16[256,256]{1,0:T(8,128)(2,1)} %constant.48.clone.ah, bf16[256,256]{1,0:T(8,128)(2,1)} %constant.49.clone.al, ...), custom_call_target="tpu_custom_call" | custom-call | flops 38654705664 | bytes 8388608 | tf_op jit(solution)/shard_map/planes/pallas_call | solution.py:462
  141.7 7.1 %last.1 = f32[1152,384]{1,0:T(8,128)} custom-call(f32[3,128,1,2304]{3,2,1,0:T(1,128)} %planes.1.r, bf16[384,400]{1,0:T(8,128)(2,1)} %constant.44.clone.gth, bf16[384,400]{1,0:T(8,128)(2,1)} %constant.45.clone.gtl, bf16[384,400]{1,0:T(8,128)(2,1)} %constant.46.clone.fth, bf16[384,400]{1,0:T(8,128)(2,1)} %constant.47.clone.ftl), custom_call_target="tpu_custom_call" | custom-call | flops 2123366400 | bytes 6291456 | tf_op jit(solution)/shard_map/last/pallas_call | solution.py:128
Async XLA Ops:
  1.7 16.8 %all-to-all-start.1 = ((f32[16,8,128]{2,1,0:T(8,128)}), f32[16,8,128]{2,1,0:T(8,128)S(1)}, u32[]{:S(2)}, u32[]{:S(2)}) async-start(f32[16,8,128]{2,1,0:T(8,128)} %prep.1), calls=%async_computation.1 | async-start | bytes 131072 | tf_op jit(solution)/shard_map/all_to_all | solution.py:511
  18.4 6.5 %copy-start.1 = (f32[16,8,128]{2,1,0:T(8,128)}, f32[16,8,128]{2,1,0:T(8,128)S(1)}, u32[]{:S(2)}) copy-start(f32[16,8,128]{2,1,0:T(8,128)S(1)} %all-to-all-done.1.got) | copy-start | bytes 196612
  18.5 27.0 %all-to-all-start = ((f32[128,1,2304]{2,1,0:T(1,128)}), f32[128,1,2304]{2,1,0:T(1,128)S(1)}, u32[]{:S(2)}, u32[]{:S(2)}) async-start(f32[128,1,2304]{2,1,0:T(1,128)} %get-tuple-element.7), calls=%async_computation | async-start | bytes 2359296 | tf_op jit(solution)/shard_map/all_to_all | solution.py:456
  45.4 1.0 copy-start

commit v3 on v2

--- a/solution.py
+++ b/solution.py
@@ -15,8 +15,7 @@
 DEV = 128
 CELLS = 1152
 PLANE = 2 * CELLS
-HEAD = 72
-TAIL = 56
+HALF = 3 * CELLS
 LIMIT = 60 * 1024 * 1024
 F32 = jnp.float32
 BF16 = jnp.bfloat16
@@ -48,39 +47,17 @@
     return mm(ah, bh, dims) + (mm(ah, bl, dims) + mm(al, bh, dims))
 
 
-def kz_first():
-    return np.arange(1, DEV + 1)
-
-
-def kz_second():
-    k = np.zeros(DEV, np.int64)
-    k[:63] = 129 + np.arange(63)
-    k[63] = 0
-    k[64] = NG // 2
-    k[65:] = 129 + np.arange(63)
-    return k
-
-
-def z_tables():
-    z = np.arange(NG)
-
-    def c(k):
-        return np.cos(2 * np.pi * ((k[:, None] * z[None]) % NG) / NG)
-
-    def s(k):
-        return np.sin(2 * np.pi * ((k[:, None] * z[None]) % NG) / NG)
-
-    first = np.concatenate([c(kz_first()), s(kz_first())])
-    k = kz_second()
-    d = np.arange(DEV)[:, None]
-    special = (d == 63) | (d == 64)
-    g_re = np.where(d < 63, c(k), 0.0)
-    g_im = np.where(d < 63, s(k), 0.0) + np.where(special, c(k), 0.0)
-    f_re = np.where(d > 62, c(k), 0.0)
-    f_im = np.where(d > 64, s(k), 0.0)
-    second_g = np.concatenate([g_re[:HEAD], g_im[:HEAD]])
-    second_f = np.concatenate([f_re[TAIL:], f_im[TAIL:]])
-    return first, second_g, second_f
+def z_table():
+    k = np.arange(1, NG // 2)[:, None] * np.arange(NG)[None]
+    angle = 2 * np.pi * (k % NG) / NG
+    c, s = np.cos(angle), np.sin(angle)
+    ends = np.stack([np.ones(NG), 1.0 - 2.0 * (np.arange(NG) % 2)])
+    return np.concatenate([c[:DEV], s[:DEV], c[DEV:], s[DEV:], ends])
+
+
+def stacked(v, axis):
+    hi, lo = cut_np(v)
+    return jnp.asarray(np.concatenate([hi, hi, lo], axis=axis))
 
 
 def mix(left, right):
@@ -170,25 +147,31 @@
     out_ref[...] = total.reshape(16, 2 * CAP, SLOTS)
 
 
-def density_body(dens, t0h, t0l, t1h, t1l, x0, y1, gh, gl):
+def density_body(dens, table, xg, g3):
     for m in range(9):
         xh, lh = m // 3, m % 3
         rows = [dens[(16 * xh + xl) * 24 + 8 * lh : (16 * xh + xl) * 24 + 8 * lh + 8, :] for xl in range(16)]
         hi, lo = cut(jnp.concatenate(rows, axis=0))
-        gh[m * 128 : (m + 1) * 128, :] = hi
-        gl[m * 128 : (m + 1) * 128, :] = lo
-    res = mm3(t0h[...], t0l[...], gh[...], gl[...], NT)
-    x0[:, 0, :CELLS] = res[:DEV]
-    x0[:, 0, CELLS:] = res[DEV:]
-    y1[...] = mm3(t1h[...], t1l[...], gh[...], gl[...], NT)
-
-
-BUFS = 4
-UNROLL = 8
-
-
-def paint_body(got, t0h, t0l, t1h, t1l, y1, x12, b0, b1, b2, b3, fh, fl):
-    bufs = (b0, b1, b2, b3)
+        at = slice(m * 128, (m + 1) * 128)
+        g3[at, :NG] = hi
+        g3[at, NG : 2 * NG] = lo
+        g3[at, 2 * NG :] = hi
+    res = mm(table[...], g3[...], NT)
+    for c in range(3):
+        xg[:, 0, c * CELLS : (c + 1) * CELLS] = res[c * DEV : (c + 1) * DEV]
+
+
+BUFS = 2
+UNROLL = 16
+
+
+def paint_body(got, table, xf, b0, b1, f3, iv, pv, cells, weights, sem):
+    bufs = (b0, b1)
+    iv[...] = got[:, CAP:].reshape(16 * CAP, SLOTS).astype(jnp.int32)
+    pv[...] = got[:, :CAP].reshape(16 * CAP, SLOTS)
+    loads = [pltpu.make_async_copy(iv, cells, sem.at[0]), pltpu.make_async_copy(pv, weights, sem.at[1])]
+    for c in loads:
+        c.start()
     zero = jnp.zeros((128, 128), F32)
 
     def clear(i, carry):
@@ -198,22 +181,22 @@
         return carry
 
     lax.fori_loop(0, 27, clear, 0)
+    for c in loads:
+        c.wait()
     lane = lax.broadcasted_iota(jnp.int32, (1, 128), 1)
 
     def one_row(r, carry):
-        src, slot = r >> 2, r & 3
-
         def more(jb):
-            return (jb < SLOTS // UNROLL) & (got[src, slot, jnp.minimum(jb * UNROLL, SLOTS - 1)] > 0.0)
+            return (jb < SLOTS // UNROLL) & (weights[r, jnp.minimum(jb * UNROLL, SLOTS - 1)] > 0.0)
 
         def step(jb):
             for u in range(UNROLL):
                 j = jb * UNROLL + u
-                at = got[src, CAP + slot, j].astype(jnp.int32)
+                at = cells[r, j]
                 b = bufs[u % BUFS]
                 row = lax.shift_right_logical(at, 7)
                 here = lane == lax.bitwise_and(at, 127)
-                b[pl.ds(row, 1), :] = b[pl.ds(row, 1), :] + jnp.where(here, got[src, slot, j], 0.0)
+                b[pl.ds(row, 1), :] = b[pl.ds(row, 1), :] + jnp.where(here, weights[r, j], 0.0)
             return jb + 1
 
         lax.while_loop(more, step, 0)
@@ -223,20 +206,15 @@
     for m in range(9):
         for zc in range(3):
             at = (zc * 9 + m) * 128
-            v = (b0[at : at + 128, :] + b1[at : at + 128, :]) + (b2[at : at + 128, :] + b3[at : at + 128, :])
-            hi, lo = cut(v)
-            fh[m * 128 : (m + 1) * 128, zc * 128 : (zc + 1) * 128] = hi
-            fl[m * 128 : (m + 1) * 128, zc * 128 : (zc + 1) * 128] = lo
-    part = mm3(t1h[...], t1l[...], fh[...], fl[...], NT)
-    for c in range(2):
-        x12[:TAIL, 0, c * CELLS : (c + 1) * CELLS] = y1[c * HEAD : c * HEAD + TAIL, :]
-        x12[TAIL:HEAD, 0, c * CELLS : (c + 1) * CELLS] = (
-            y1[c * HEAD + TAIL : (c + 1) * HEAD, :] + part[c * HEAD : c * HEAD + HEAD - TAIL]
-        )
-        x12[HEAD:, 0, c * CELLS : (c + 1) * CELLS] = part[c * HEAD + HEAD - TAIL : (c + 1) * HEAD]
-    res = mm3(t0h[...], t0l[...], fh[...], fl[...], NT)
-    x12[:, 0, PLANE : PLANE + CELLS] = res[:DEV]
-    x12[:, 0, PLANE + CELLS :] = res[DEV:]
+            hi, lo = cut(b0[at : at + 128, :] + b1[at : at + 128, :])
+            rows = slice(m * 128, (m + 1) * 128)
+            f3[rows, zc * 128 : (zc + 1) * 128] = hi
+            f3[rows, NG + zc * 128 : NG + (zc + 1) * 128] = lo
+            f3[rows, 2 * NG + zc * 128 : 2 * NG + (zc + 1) * 128] = hi
+    res = mm(table[...], f3[...], NT)
+    xf[0, :, 0, :] = res[2 * DEV :]
+    xf[1, :, 0, :] = res[:DEV]
+    xf[2, :, 0, :] = res[DEV : 2 * DEV]
 
 
 ROOT = 0.8660254037844386
@@ -290,68 +268,66 @@
     lax.fori_loop(1, DEV, step, 0)
 
 
-def fill_window(me, win):
-    second = jnp.where(me < 63, 129 + me, jnp.where(me == 63, 0, jnp.where(me == 64, NG // 2, 64 + me)))
+def fill_window(k, which, win):
     lane = lax.broadcasted_iota(jnp.int32, (RB, 128), 1)
     sub = lax.broadcasted_iota(jnp.int32, (RB, 128), 0)
-    for which, k in ((0, me + 1), (1, second)):
-        scale = jnp.where((k == 0) | (k == NG // 2), 1.0, 2.0) / float(NG) ** 3
-        fz = signed(k)
-
-        def step(i, carry):
-            m, r = i // (DEV // RB), i % (DEV // RB)
-            s = sub + r * RB
-            bx = m // 3
-            kx = (s >> 4) + 8 * bx + 24 * (lane >> 3)
-            ky = (s & 15) + 16 * (m - 3 * bx) + 48 * (lane & 7)
-            value = top_hat(signed(kx), signed(ky), fz) * scale
-            win[which, pl.ds(pl.multiple_of(i * RB, RB), RB), :] = value
-            return carry
-
-        lax.fori_loop(0, CELLS // RB, step, 0)
+    scale = jnp.where((k == 0) | (k == NG // 2), 1.0, 2.0) / float(NG) ** 3
+    fz = signed(k)
+
+    def step(i, carry):
+        m, r = i // (DEV // RB), i % (DEV // RB)
+        s = sub + r * RB
+        bx = m // 3
+        kx = (s >> 4) + 8 * bx + 24 * (lane >> 3)
+        ky = (s & 15) + 16 * (m - 3 * bx) + 48 * (lane & 7)
+        value = top_hat(signed(kx), signed(ky), fz) * scale
+        win[which, pl.ds(pl.multiple_of(i * RB, RB), RB), :] = value
+        return carry
+
+    lax.fori_loop(0, CELLS // RB, step, 0)
 
 
 def planes_body(
-    x0, x12, tw_hbm, ah, al, bh, bl, ch, cl, dh, dl, out,
+    xg, xf, tw_hbm, ah, al, bh, bl, ch, cl, dh, dl, out,
     xs, ys, win, tw, wide, tall, uh, ul, vh, vl, sx, rx, sy, ry, own, sl,
 ):
     px, py = lax.axis_index("px"), lax.axis_index("py")
     me = px * 16 + py
-    loads = [
-        pltpu.make_async_copy(x0, xs.at[0], sl.at[0]),
-        pltpu.make_async_copy(tw_hbm, tw, sl.at[1]),
-    ]
-    for q in range(2):
-        mine = x12.at[me, :, pl.ds(q * PLANE, PLANE)]
-        loads.append(pltpu.make_async_copy(mine, xs.at[q + 1, me], sl.at[2 + q]))
+    loads = [pltpu.make_async_copy(tw_hbm, tw, sl.at[0])]
+    for c in range(3):
+        loads.append(pltpu.make_async_copy(xg.at[:, :, pl.ds(c * CELLS, CELLS)], xs.at[c], sl.at[1 + c]))
+        loads.append(pltpu.make_async_copy(xf.at[c, me], xs.at[3 + c, me], sl.at[4 + c]))
     for c in loads:
         c.start()
     barrier = pltpu.get_barrier_semaphore()
     everyone(lambda a, b: pl.semaphore_signal(barrier, inc=1, device_id=(a, b), device_id_type=MESH))
     pl.semaphore_wait(barrier, DEV - 1)
-    for q in range(2):
+    pieces = ((0, 1), (1, 2))
+    for q, (start, size) in enumerate(pieces):
         everyone(
             lambda a, b: pltpu.make_async_remote_copy(
-                src_ref=x12.at[a * 16 + b, :, pl.ds(q * PLANE, PLANE)],
-                dst_ref=xs.at[q + 1, me],
+                src_ref=xf.at[pl.ds(start, size), a * 16 + b],
+                dst_ref=xs.at[pl.ds(3 + start, size), me],
                 send_sem=sx.at[q],
                 recv_sem=rx.at[q],
                 device_id=(a, b),
                 device_id_type=MESH,
             ).start()
         )
-    fill_window(me, win)
+    fill_window(me + 1, 0, win)
     for c in loads:
         c.wait()
 
     def one_plane(p, carry):
-        @pl.when(p > 0)
-        def _():
-            part = xs.at[p, pl.ds(0, DEV - 1)]
-            pltpu.make_async_copy(part, part, rx.at[p - 1]).wait()
+        for q, (start, size) in enumerate(pieces):
+
+            @pl.when(p == q + 1)
+            def _():
+                part = xs.at[pl.ds(3 + start, size), pl.ds(0, DEV - 1)]
+                pltpu.make_async_copy(part, part, rx.at[q]).wait()
 
         for c in range(2):
-            wide[c * DEV : (c + 1) * DEV, :] = xs[p, :, 0, c * CELLS : (c + 1) * CELLS]
+            wide[c * DEV : (c + 1) * DEV, :] = xs[2 * p + c, :, 0, :]
         hi, lo = cut(wide[...])
         wide[...] = mm3(ah[...], al[...], hi, lo)
 
@@ -412,11 +388,17 @@
                 device_id_type=MESH,
             ).start()
         )
+
+        @pl.when(p == 0)
+        def _():
+            second = jnp.where(me < 63, 129 + me, jnp.where(me < 126, 66 + me, (me - 126) * (NG // 2)))
+            fill_window(second, 1, win)
+
         return carry
 
     lax.fori_loop(0, 3, one_plane, 0)
-    for q in range(2):
-        part = x12.at[pl.ds(0, DEV - 1), :, pl.ds(q * PLANE, PLANE)]
+    for q, (start, size) in enumerate(pieces):
+        part = xf.at[pl.ds(start, size), pl.ds(0, DEV - 1)]
         pltpu.make_async_copy(part, part, sx.at[q]).wait()
     for p in range(3):
         part = ys.at[p, pl.ds(0, DEV - 1)]
@@ -425,19 +407,16 @@
         pltpu.make_async_copy(part, part, ry.at[p]).wait()
 
 
-def last_body(r, gth, gtl, fth, ftl, out, stack, ga, fa):
-    for c in range(2):
-        cols = slice(c * CELLS, (c + 1) * CELLS)
-        stack[c * DEV : (c + 1) * DEV, :] = r[0, :, 0, cols]
-        stack[2 * DEV + c * HEAD : 2 * DEV + (c + 1) * HEAD, :] = r[1, :HEAD, 0, cols]
-    hi, lo = cut(stack[...])
-    ga[...] = mm3(gth[...], gtl[...], hi, lo)
-    for c in range(2):
-        cols = slice(c * CELLS, (c + 1) * CELLS)
-        stack[c * DEV : (c + 1) * DEV, :] = r[2, :, 0, cols]
-        stack[2 * DEV + c * HEAD : 2 * DEV + (c + 1) * HEAD, :] = r[1, TAIL:, 0, cols]
-    hi, lo = cut(stack[...])
-    fa[...] = mm3(fth[...], ftl[...], hi, lo)
+def last_body(r, table, out, stack, ga, fa):
+    parts = (((0, 0), (0, 1), (1, 0)), ((2, 0), (2, 1), (1, 1)))
+    for result, rows in zip((ga, fa), parts):
+        for i, (p, c) in enumerate(rows):
+            result[i * DEV : (i + 1) * DEV, :] = r[p, :, 0, c * CELLS : (c + 1) * CELLS]
+        hi, lo = cut(result[...])
+        stack[:NG, :] = hi
+        stack[NG : 2 * NG, :] = lo
+        stack[2 * NG :, :] = hi
+        result[...] = mm(table[...], stack[...], NN)
     for m in range(9):
         xh, lh = m // 3, m % 3
         cols = slice(m * 128, (m + 1) * 128)
@@ -456,7 +435,7 @@
     return lax.all_to_all(a, ("px", "py"), split_axis=0, concat_axis=0, tiled=True)
 
 
-def planes(x0, x12, tw, mats):
+def planes(xg, xf, tw, mats):
     dma = pltpu.SemaphoreType.DMA
     plane = (DEV, 1, PLANE)
     return pl.pallas_call(
@@ -465,7 +444,7 @@
         in_specs=[pl.BlockSpec(memory_space=pl.ANY)] * 3 + [pl.BlockSpec(memory_space=VMEM)] * 8,
         out_specs=pl.BlockSpec(memory_space=pl.ANY),
         scratch_shapes=[
-            VMEM((3, *plane), F32),
+            VMEM((6, DEV, 1, CELLS), F32),
             VMEM((3, *plane), F32),
             VMEM((2, CELLS, 128), F32),
             VMEM((4, CELLS, 128), F32),
@@ -480,21 +459,17 @@
             dma((3,)),
             dma((3,)),
             dma,
-            dma((4,)),
+            dma((7,)),
         ],
         compiler_params=pltpu.CompilerParams(vmem_limit_bytes=LIMIT, collective_id=1, has_side_effects=True),
         cost_estimate=pl.CostEstimate(flops=36 << 30, bytes_accessed=8 << 20, transcendentals=0),
         name="planes",
-    )(x0, x12, tw, *mats)
+    )(xg, xf, tw, *mats)
 
 
 def on_device(photons, halo_cells, halo_counts, owners, density):
-    first, second_g, second_f = z_tables()
-    t0 = [jnp.asarray(t) for t in cut_np(first)]
-    t1g = [jnp.asarray(t) for t in cut_np(second_g)]
-    t1f = [jnp.asarray(t) for t in cut_np(second_f)]
-    back_g = [jnp.asarray(t) for t in cut_np(np.concatenate([first, second_g]).T)]
-    back_f = [jnp.asarray(t) for t in cut_np(np.concatenate([first, second_f]).T)]
+    table = z_table()
+    ahead, back = stacked(table, 1), stacked(table.T, 1)
     mats = []
     for m in (row_matrix(1), row_matrix(-1), lane_matrix(1), lane_matrix(-1)):
         mats += [jnp.asarray(t) for t in cut_np(m)]
@@ -509,32 +484,35 @@
         name="prep",
     )
     got = lax.all_to_all(send, "py", split_axis=0, concat_axis=0, tiled=True)
-    x0, y1 = call(
+    xg = call(
         density_body,
-        (sds(DEV, 1, PLANE), sds(2 * HEAD, CELLS)),
-        (density.reshape(CELLS, NG), *t0, *t1g),
-        [VMEM((CELLS, NG), BF16)] * 2,
+        sds(DEV, 1, HALF),
+        (density.reshape(CELLS, NG), ahead),
+        [VMEM((CELLS, 3 * NG), BF16)],
         flops=6 * 400 * NG * CELLS,
         nbytes=4 << 20,
         name="density",
     )
-    x0 = exchange(x0)
-    x12 = call(
+    xg = exchange(xg)
+    xf = call(
         paint_body,
-        sds(DEV, 1, 2 * PLANE),
-        (got, *t0, *t1f, y1),
-        [VMEM((3 * CELLS, 128), F32)] * BUFS + [VMEM((CELLS, NG), BF16)] * 2,
-        spaces=[SMEM] + [VMEM] * 5,
+        sds(3, DEV, 1, CELLS),
+        (got, ahead),
+        [VMEM((3 * CELLS, 128), F32)] * BUFS
+        + [VMEM((CELLS, 3 * NG), BF16)]
+        + [VMEM((16 * CAP, SLOTS), jnp.int32), VMEM((16 * CAP, SLOTS), F32)]
+        + [SMEM((16 * CAP, SLOTS), jnp.int32), SMEM((16 * CAP, SLOTS), F32)]
+        + [pltpu.SemaphoreType.DMA((2,))],
         flops=6 * 400 * NG * CELLS * 3,
         nbytes=4 << 20,
         name="paint",
     )
-    r = planes(x0, x12, jnp.asarray(twiddles()), mats)
+    r = planes(xg, xf, jnp.asarray(twiddles()), mats)
     out = call(
         last_body,
         sds(CELLS, NG),
-        (r, *back_g, *back_f),
-        [VMEM((400, CELLS), F32), VMEM((NG, CELLS), F32), VMEM((NG, CELLS), F32)],
+        (r, back),
+        [VMEM((3 * NG, CELLS), BF16), VMEM((NG, CELLS), F32), VMEM((NG, CELLS), F32)],
         flops=6 * 2 * 400 * NG * CELLS,
         nbytes=6 << 20,
         name="last",

time: 150 us -> 129 us (0.86)
  Pallas kernels: 129 us -> 95.9 us
  waiting for transfers between devices: 3.14 us -> 15.3 us
    pallas_call x1, Pallas kernels: 95.2 us -> 68.8 us  [planes(): pl.pallas_call(planes_body, out_shape=sds(3, *plane), in_specs=[pl.BlockS...]
    all_to_all x1, waiting for transfers between devices: 0.39 us -> 12.5 us  [exchange(): lax.all_to_all(a, ('px', 'py'), split_axis=0, concat_axis=0, tiled=True)]
    pallas_call x4, Pallas kernels: 33.4 us -> 27 us  [call(): pl.pallas_call(body, out_shape=out_shape, in_specs=[pl.BlockSpec(memory_s...]
  transfers between devices with their start and end apart: 2 -> 2, of which waited for: 2 -> 2; matrix products, arithmetic and copies ran while one was open for 0% -> 0% of each run, Pallas kernels for 17% -> 15%
where the time goes in v3:
time: 129 us
  Pallas kernels  95.9 us (74%)
  starting transfers between devices  16 us (12%)
  waiting for transfers between devices  15.3 us (12%)
  local copies, waits for them, and re-layouts  1.82 us (1%)
    pallas_call x1, Pallas kernels, planes(): pl.pallas_call(planes_body, out_shape=sds(3, *plane), in_specs=[pl.BlockS...  68.8 us
    pallas_call x4, Pallas kernels, call(): pl.pallas_call(body, out_shape=out_shape, in_specs=[pl.BlockSpec(memory_s...  27 us
    all_to_all x1, waiting for transfers between devices, exchange(): lax.all_to_all(a, ('px', 'py'), split_axis=0, concat_axis=0, tiled=True)  12.5 us
    all_to_all x1, starting transfers between devices, on_device(): got = lax.all_to_all(send, 'py', split_axis=0, concat_axis=0, tiled=True)  9.45 us
    all_to_all x1, starting transfers between devices, exchange(): lax.all_to_all(a, ('px', 'py'), split_axis=0, concat_axis=0, tiled=True)  6.51 us
    all_to_all x1, waiting for transfers between devices, on_device(): got = lax.all_to_all(send, 'py', split_axis=0, concat_axis=0, tiled=True)  2.75 us
  transfers between devices with their start and end apart: 2, of which 2 were waited for; matrix products, arithmetic and copies ran while one was open for 0% of the time, Pallas kernels for 15%

profile of v3, /device:TPU:1, one launch (start us, length us, event | category | flops | bytes accessed | tf_op | source)
XLA Modules:
  0.0 129.0 jit_solution(11905624808645495413)
XLA Ops:
  0.0 1.7 %prep.1 = f32[16,8,128]{2,1,0:T(8,128)} custom-call(f32[32,128]{1,0:T(8,128)} %ph_ref.1, s32[32,128]{1,0:T(8,128)} %cell_ref.1, s32[1,32]{1,0:T(1,128)} %bitcast.5, s32[1,32]{1,0:T(1,128)} %bitcast.6), custom_call_target="tpu_custom_call" | custom-call | flops 1048576 | bytes 131072 | tf_op jit(solution)/shard_map/prep/pallas_call | solution.py:105
  1.7 9.4 %all-to-all-start.1 = ((f32[16,8,128]{2,1,0:T(8,128)}), f32[16,8,128]{2,1,0:T(8,128)S(1)}, u32[]{:S(2)}, u32[]{:S(2)}) async-start(f32[16,8,128]{2,1,0:T(8,128)} %prep.1), calls=%async_computation.1 | async-start | bytes 131072 | tf_op jit(solution)/shard_map/all_to_all | solution.py:486
  11.1 4.6 %density.1 = f32[128,1,3456]{2,1,0:T(1,128)} custom-call(f32[1152,384]{1,0:T(8,128)} %bitcast.4, bf16[384,1152]{1,0:T(8,128)(2,1)} %constant.22.clone.table), custom_call_target="tpu_custom_call" | custom-call | flops 1061683200 | bytes 4194304 | tf_op jit(solution)/shard_map/density/pallas_call | solution.py:105
  15.7 2.8 %all-to-all-done.1.got = f32[16,8,128]{2,1,0:T(8,128)S(1)} async-done(((f32[16,8,128]{2,1,0:T(8,128)}), f32[16,8,128]{2,1,0:T(8,128)S(1)}, u32[]{:S(2)}, u32[]{:S(2)}) %all-to-all-start.1) | async-done | bytes 65568 | tf_op jit(solution)/shard_map/all_to_all | solution.py:486
  18.4 0.0 copy-start.1
  18.5 0.6 copy-done.1
  19.1 6.5 %all-to-all-start = ((f32[128,1,3456]{2,1,0:T(1,128)}), f32[128,1,3456]{2,1,0:T(1,128)S(1)}, u32[]{:S(2)}, u32[]{:S(2)}) async-start(f32[128,1,3456]{2,1,0:T(1,128)} %density.1), calls=%async_computation | async-start | bytes 3538944 | tf_op jit(solution)/shard_map/all_to_all | solution.py:435
  25.6 14.2 %paint.1.xf = f32[3,128,1,1152]{3,2,1,0:T(1,128)} custom-call(f32[16,8,128]{2,1,0:T(8,128)} %copy-done.1, bf16[384,1152]{1,0:T(8,128)(2,1)} %constant.22.clone.table), custom_call_target="tpu_custom_call" | custom-call | flops 3185049600 | bytes 4194304 | tf_op jit(solution)/shard_map/paint/pallas_call | solution.py:105
  39.8 12.5 %all-to-all-done.xg = f32[128,1,3456]{2,1,0:T(1,128)S(1)} async-done(((f32[128,1,3456]{2,1,0:T(1,128)}), f32[128,1,3456]{2,1,0:T(1,128)S(1)}, u32[]{:S(2)}, u32[]{:S(2)}) %all-to-all-start) | async-done | bytes 1769504 | tf_op jit(solution)/shard_map/all_to_all | solution.py:435
  52.3 0.0 copy-start
  52.3 1.2 copy-done
  53.5 68.8 %planes.1.r = f32[3,128,1,2304]{3,2,1,0:T(1,128)} custom-call(f32[128,1,3456]{2,1,0:T(1,128)} %copy-done, f32[3,128,1,1152]{3,2,1,0:T(1,128)} %paint.1.xf, f32[4,1152,128]{2,1,0:T(8,128)} %constant.32.clone.tw_hbm, bf16[256,256]{1,0:T(8,128)(2,1)} %constant.24.clone.ah, bf16[256,256]{1,0:T(8,128)(2,1)} %constant.25.clone.al, ...), custom_call_target="tpu_custom_call" | custom-call | flops 38654705664 | bytes 8388608 | tf_op jit(solution)/shard_map/planes/pallas_call | solution.py:441
  122.4 6.6 %last.1 = f32[1152,384]{1,0:T(8,128)} custom-call(f32[3,128,1,2304]{3,2,1,0:T(1,128)} %planes.1.r, bf16[384,1152]{1,0:T(8,128)(2,1)} %constant.23.clone.table), custom_call_target="tpu_custom_call" | custom-call | flops 2123366400 | bytes 6291456 | tf_op jit(solution)/shard_map/last/pallas_call | solution.py:105
Async XLA Ops:
  1.7 16.8 %all-to-all-start.1 = ((f32[16,8,128]{2,1,0:T(8,128)}), f32[16,8,128]{2,1,0:T(8,128)S(1)}, u32[]{:S(2)}, u32[]{:S(2)}) async-start(f32[16,8,128]{2,1,0:T(8,128)} %prep.1), calls=%async_computation.1 | async-start | bytes 131072 | tf_op jit(solution)/shard_map/all_to_all | solution.py:486
  18.4 0.6 copy-start.1
  19.1 33.3 %all-to-all-start = ((f32[128,1,3456]{2,1,0:T(1,128)}), f32[128,1,3456]{2,1,0:T(1,128)S(1)}, u32[]{:S(2)}, u32[]{:S(2)}) async-start(f32[128,1,3456]{2,1,0:T(1,128)} %density.1), calls=%async_computation | async-start | bytes 3538944 | tf_op jit(solution)/shard_map/all_to_all | solution.py:435
  52.3 1.2 copy-start

commit v4 on v3

v4 whole, which is shorter than its diff:
```python
import functools

import jax
import jax.numpy as jnp
import numpy as np
from jax import lax
from jax.experimental import pallas as pl
from jax.experimental.pallas import tpu as pltpu
from jax.sharding import PartitionSpec as P

NG = 384
SLOTS = 128
CAP = 4
RADIUS = 20
DEV = 128
CELLS = 1152
PLANE = 2 * CELLS
HALF = 3 * CELLS
LIMIT = 60 * 1024 * 1024
F32 = jnp.float32
BF16 = jnp.bfloat16
VMEM = pltpu.VMEM
MESH = pl.DeviceIdType.MESH


def cut(v):
    hi = v.astype(BF16)
    return hi, (v - hi.astype(F32)).astype(BF16)


def cut_np(v):
    v = np.asarray(v, np.float32)
    hi = v.astype(jnp.bfloat16)
    lo = (v - hi.astype(np.float32)).astype(jnp.bfloat16)
    return hi, lo


NN = (((1,), (0,)), ((), ()))
NT = (((1,), (1,)), ((), ()))


def mm(a, b, dims):
    return lax.dot_general(a, b, dims, preferred_element_type=F32)


def mm3(ah, al, bh, bl, dims=NN):
    return mm(ah, bh, dims) + (mm(ah, bl, dims) + mm(al, bh, dims))


def z_table():
    k = np.arange(1, NG // 2)[:, None] * np.arange(NG)[None]
    angle = 2 * np.pi * (k % NG) / NG
    c, s = np.cos(angle), np.sin(angle)
    ends = np.stack([np.ones(NG), 1.0 - 2.0 * (np.arange(NG) % 2)])
    return np.concatenate([c[:DEV], s[:DEV], c[DEV:], s[DEV:], ends])


def stacked(v, axis):
    hi, lo = cut_np(v)
    return jnp.asarray(np.concatenate([hi, hi, lo], axis=axis))


def mix(left, right):
    i = np.arange(left * right)
    a, b = i // right, i % right
    ph = -2j * np.pi * (np.outer(a, a) / left + np.outer(b, b) / right)
    return np.exp(ph)


def row_matrix(sign):
    m = mix(8, 16)
    re, im = m.real, sign * m.imag
    return np.block([[re, -im], [im, re]])


def lane_matrix(sign):
    m = mix(16, 8)
    re, im = m.real, sign * m.imag
    return np.block([[re, im], [-im, re]])


def twiddles():
    row, lane = np.arange(CELLS)[:, None], np.arange(128)[None]
    m, s = row // 128, row % 128
    ax, ay, bx, by, cx, cy = s // 16, s % 16, m // 3, m % 3, lane // 8, lane % 8
    one = (ax * bx * 16 + ay * by * 8 + 0 * lane) * (2 * np.pi / NG)
    two = (cx * (ax + 8 * bx) + cy * (ay + 16 * by)) * (2 * np.pi / NG)
    return np.stack([np.cos(one), -np.sin(one), np.cos(two), -np.sin(two)]).astype(np.float32)


def signed(k):
    return jnp.where(k < NG // 2, k, k - NG).astype(F32)


def top_hat(freq_x, freq_y, freq_z):
    radial = jnp.sqrt(freq_x * freq_x + freq_y * freq_y + freq_z * freq_z) * (2.0 * jnp.pi * RADIUS / NG)
    safe = jnp.where(radial > 0, radial, 1.0)
    value = 3.0 * (jnp.sin(safe) - safe * jnp.cos(safe)) / (safe * safe * safe)
    return jnp.where(radial > 0, value, 1.0)


def pack(photons, cells, counts, owned):
    lane = lax.broadcasted_iota(jnp.int32, (32, SLOTS), 1)
    first = lax.broadcasted_iota(jnp.int32, (32, 32), 0)
    second = lax.broadcasted_iota(jnp.int32, (32, 32), 1)

    def column(row):
        spread = jnp.where(first == second, row.astype(F32), 0.0)
        return jnp.sum(spread, axis=1, keepdims=True).astype(jnp.int32)

    live = lane < column(counts)
    w = jnp.where(live, photons, 0.0)
    cell = jnp.where(live, cells, 0)
    column_of = cell // NG
    gz = cell - column_of * NG
    gx = column_of // 24
    gy = column_of - gx * 24
    place_in = ((gx >> 4) * 3 + (gy >> 3)) * 128 + (gx & 15) * 8 + (gy & 7)
    spot = (place_in * 512 + gz).astype(F32)
    same = (column(owned) == owned) & (first < second)
    rank = jnp.sum(jnp.where(same, 1.0, 0.0), axis=0, keepdims=True).astype(jnp.int32)
    place = owned * (2 * CAP) + rank
    rows = lax.broadcasted_iota(jnp.int32, (DEV, 32), 0)
    total = jnp.zeros((DEV, SLOTS), F32)
    for values, shift in ((w, 0), (spot, CAP)):
        hot = jnp.where(rows == place + shift, 1.0, 0.0).astype(BF16)
        hi = values.astype(BF16)
        rest = values - hi.astype(F32)
        mid = rest.astype(BF16)
        low = (rest - mid.astype(F32)).astype(BF16)
        total = total + ((mm(hot, hi, NN) + mm(hot, mid, NN)) + mm(hot, low, NN))
    return total.reshape(16, 2 * CAP, SLOTS)


KR = 16
STEP = KR * SLOTS


def one_hots(land, zp, col):
    spot = land[:, CAP:].reshape(16 * CAP, SLOTS).astype(jnp.int32)
    weight = land[:, :CAP].reshape(16 * CAP, SLOTS)
    hi = weight.astype(BF16).astype(F32)
    lo = weight - hi
    z = spot & 511
    col[...] = spot >> 9
    rows = lax.broadcasted_iota(jnp.int32, (NG, SLOTS), 0)
    for r in range(16 * CAP):
        hit = rows == z[r : r + 1, :]
        at = slice(r * SLOTS, (r + 1) * SLOTS)
        zp[:NG, at] = jnp.where(hit, hi[r : r + 1, :], 0.0).astype(BF16)
        zp[NG:, at] = jnp.where(hit, lo[r : r + 1, :], 0.0).astype(BF16)


def paint_group(g, zp, col, spread, acc):
    rows = lax.broadcasted_iota(jnp.int32, (NG, SLOTS), 0) + g * NG
    for kk in range(16 * CAP // KR):
        for r in range(KR):
            hit = rows == col[kk * KR + r : kk * KR + r + 1, :]
            spread[:, r * SLOTS : (r + 1) * SLOTS] = jnp.where(hit, 1.0, 0.0).astype(BF16)
        both = mm(zp[:, kk * STEP : (kk + 1) * STEP], spread[...], NT)
        part = both[:NG] + both[NG:]
        if kk == 0:
            acc[...] = part
        else:
            acc[...] += part


ROOT = 0.8660254037844386


def three(a, b, c, inverse):
    tr, ti = b[0] + c[0], b[1] + c[1]
    dr, di = ROOT * (b[0] - c[0]), ROOT * (b[1] - c[1])
    er, ei = a[0] - 0.5 * tr, a[1] - 0.5 * ti
    one, two = (er + di, ei - dr), (er - di, ei + dr)
    return (a[0] + tr, a[1] + ti), *((two, one) if inverse else (one, two))


def nine(v, inverse):
    v = list(v)
    for x in range(3):
        v[3 * x : 3 * x + 3] = three(*v[3 * x : 3 * x + 3], inverse)
    for y in range(3):
        v[y], v[y + 3], v[y + 6] = three(v[y], v[y + 3], v[y + 6], inverse)
    return v


def turn(v, c, s):
    return v[0] * c - v[1] * s, v[0] * s + v[1] * c


RB = 16
def coords():
    px, py = lax.axis_index("px"), lax.axis_index("py")
    return px & 3, ((py >> 1) & 1) * 2 + (px >> 2), py >> 2, py & 1


def partner(t):
    x, y, z, core = coords()
    u = (t * 101) & 127
    sign = 1 - 2 * core
    x2 = (x + sign * ((u >> 1) & 3)) & 3
    y2 = (y + sign * ((u >> 3) & 3)) & 3
    z2 = (z + sign * ((u >> 5) & 3)) & 3
    return (y2 & 1) * 4 + x2, z2 * 4 + (y2 >> 1) * 2 + ((core + u) & 1)


def everyone(body):
    def step(t, carry):
        body(*partner(t))
        return carry

    lax.fori_loop(1, DEV, step, 0)


def fill_window(k, which, win):
    lane = lax.broadcasted_iota(jnp.int32, (RB, 128), 1)
    sub = lax.broadcasted_iota(jnp.int32, (RB, 128), 0)
    scale = jnp.where((k == 0) | (k == NG // 2), 1.0, 2.0) / float(NG) ** 3
    fz = signed(k)

    def step(i, carry):
        m, r = i // (DEV // RB), i % (DEV // RB)
        s = sub + r * RB
        bx = m // 3
        kx = (s >> 4) + 8 * bx + 24 * (lane >> 3)
        ky = (s & 15) + 16 * (m - 3 * bx) + 48 * (lane & 7)
        value = top_hat(signed(kx), signed(ky), fz) * scale
        win[which, pl.ds(pl.multiple_of(i * RB, RB), RB), :] = value
        return carry

    lax.fori_loop(0, CELLS // RB, step, 0)


def whole_body(
    ph, cell, count, owned, dens_hbm, table_hbm, tw_hbm, back_hbm, ah, al, bh, bl, ch, cl, dh, dl, out, ga_hbm, fa_hbm,
    dens, table, send, land, zp, col, spread, acc, f3, xg, xf, gs, fs,
    ys, rb, win, tw, back, ga, fa, stack, wide, tall, uh, ul, vh, vl, ss, rs, sg, rg, sf, rf, sy, ry, own, sl,
):
    px, py = lax.axis_index("px"), lax.axis_index("py")
    me = px * 16 + py
    loads = [
        pltpu.make_async_copy(a, b, sl.at[i])
        for i, (a, b) in enumerate(((dens_hbm, dens), (table_hbm, table), (tw_hbm, tw), (back_hbm, back)))
    ]
    for c in loads:
        c.start()
    barrier = pltpu.get_barrier_semaphore()
    everyone(lambda a, b: pl.semaphore_signal(barrier, inc=1, device_id=(a, b), device_id_type=MESH))
    send[...] = pack(ph[...], cell[...], count[...], owned[...])
    mine = pltpu.make_async_copy(send.at[py], land.at[py], own)
    mine.start()
    mine.wait()
    loads[0].wait()
    for m in range(9):
        xh, lh = m // 3, m % 3
        rows = [dens[(16 * xh + xl) * 24 + 8 * lh : (16 * xh + xl) * 24 + 8 * lh + 8, :] for xl in range(16)]
        hi, lo = cut(jnp.concatenate(rows, axis=0))
        at = slice(m * 128, (m + 1) * 128)
        stack[at, :NG] = hi
        stack[at, NG : 2 * NG] = lo
        stack[at, 2 * NG :] = hi
    pl.semaphore_wait(barrier, DEV - 1)
    for t in range(1, 16):
        to = (py + t) & 15
        pltpu.make_async_remote_copy(
            src_ref=send.at[to],
            dst_ref=land.at[py],
            send_sem=ss,
            recv_sem=rs,
            device_id=(px, to),
            device_id_type=MESH,
        ).start()
    loads[1].wait()
    res = mm(table[...], stack[...], NT)
    for c in range(3):
        xg[:, 0, c * CELLS : (c + 1) * CELLS] = res[c * DEV : (c + 1) * DEV]
    mine = pltpu.make_async_copy(xg.at[me], gs.at[me], own)
    mine.start()
    mine.wait()
    everyone(
        lambda a, b: pltpu.make_async_remote_copy(
            src_ref=xg.at[a * 16 + b],
            dst_ref=gs.at[me],
            send_sem=sg,
            recv_sem=rg,
            device_id=(a, b),
            device_id_type=MESH,
        ).start()
    )
    part = land.at[pl.ds(0, 15)]
    pltpu.make_async_copy(part, part, rs).wait()
    one_hots(land, zp, col)

    def one_group(g, carry):
        paint_group(g, zp, col, spread, acc)
        hi, lo = cut(acc[...])
        f3[:NG, :] = hi
        f3[NG : 2 * NG, :] = lo
        f3[2 * NG :, :] = hi
        res = mm(table[...], f3[...], NN)
        for c, first in enumerate((2 * DEV, 0, DEV)):
            xf[g, :, 0, c * NG : (c + 1) * NG] = res[first : first + DEV]
        mine = pltpu.make_async_copy(xf.at[g, me], fs.at[g, me], own)
        mine.start()
        mine.wait()
        everyone(
            lambda a, b: pltpu.make_async_remote_copy(
                src_ref=xf.at[g, a * 16 + b],
                dst_ref=fs.at[g, me],
                send_sem=sf.at[g],
                recv_sem=rf.at[g],
                device_id=(a, b),
                device_id_type=MESH,
            ).start()
        )
        return carry

    lax.fori_loop(0, 3, one_group, 0)
    fill_window(me + 1, 0, win)
    for c in loads[2:]:
        c.wait()
    part = gs.at[pl.ds(0, DEV - 1)]
    pltpu.make_async_copy(part, part, rg).wait()

    def one_plane(p, carry):
        @pl.when(p == 0)
        def _():
            for c in range(2):
                wide[c * DEV : (c + 1) * DEV, :] = gs[:, 0, c * CELLS : (c + 1) * CELLS]

        @pl.when(p == 1)
        def _():
            for g in range(3):
                part = fs.at[g, pl.ds(0, DEV - 1)]
                pltpu.make_async_copy(part, part, rf.at[g]).wait()
            wide[:DEV, :] = gs[:, 0, 2 * CELLS :]
            for g in range(3):
                wide[DEV:, g * NG : (g + 1) * NG] = fs[g, :, 0, :NG]

        @pl.when(p == 2)
        def _():
            for c in range(2):
                for g in range(3):
                    wide[c * DEV : (c + 1) * DEV, g * NG : (g + 1) * NG] = fs[g, :, 0, (c + 1) * NG : (c + 2) * NG]

        hi, lo = cut(wide[...])
        wide[...] = mm3(ah[...], al[...], hi, lo)

        def forward(i, inner):
            r = pl.multiple_of(i * RB, RB)
            v = []
            for m in range(9):
                cols = slice(m * 128, (m + 1) * 128)
                t = pl.ds(m * 128 + r, RB)
                u = (wide[pl.ds(r, RB), cols], wide[pl.ds(DEV + r, RB), cols])
                v.append(turn(u, tw[0, t, :], tw[1, t, :]))
            for m, u in enumerate(nine(v, False)):
                t = pl.ds(m * 128 + r, RB)
                for c, part in enumerate(turn(u, tw[2, t, :], tw[3, t, :])):
                    hi, lo = cut(part)
                    uh[t, c * 128 : (c + 1) * 128] = hi
                    ul[t, c * 128 : (c + 1) * 128] = lo
            return inner

        lax.fori_loop(0, DEV // RB, forward, 0)
        mid = mm3(uh[...], ul[...], ch[...], cl[...])
        this = win[p & 1]
        for c in range(2):
            hi, lo = cut(mid[:, c * 128 : (c + 1) * 128] * this)
            uh[:, c * 128 : (c + 1) * 128] = hi
            ul[:, c * 128 : (c + 1) * 128] = lo
        tall[...] = mm3(uh[...], ul[...], dh[...], dl[...])

        def backward(i, inner):
            r = pl.multiple_of(i * RB, RB)
            v = []
            for m in range(9):
                t = pl.ds(m * 128 + r, RB)
                v.append(turn((tall[t, :128], tall[t, 128:]), tw[2, t, :], -tw[3, t, :]))
            for m, u in enumerate(nine(v, True)):
                t = pl.ds(m * 128 + r, RB)
                cols = slice(m * 128, (m + 1) * 128)
                for c, part in enumerate(turn(u, tw[0, t, :], -tw[1, t, :])):
                    hi, lo = cut(part)
                    vh[pl.ds(c * DEV + r, RB), cols] = hi
                    vl[pl.ds(c * DEV + r, RB), cols] = lo
            return inner

        lax.fori_loop(0, DEV // RB, backward, 0)
        back = mm3(bh[...], bl[...], vh[...], vl[...])
        for c in range(2):
            ys[p, :, 0, c * CELLS : (c + 1) * CELLS] = back[c * DEV : (c + 1) * DEV]
        def give(home, q):
            mine = pltpu.make_async_copy(ys.at[p, me], home.at[q, me], own)
            mine.start()
            mine.wait()
            everyone(
                lambda a, b: pltpu.make_async_remote_copy(
                    src_ref=ys.at[p, a * 16 + b],
                    dst_ref=home.at[q, me],
                    send_sem=sy.at[p],
                    recv_sem=ry.at[p],
                    device_id=(a, b),
                    device_id_type=MESH,
                ).start()
            )

        @pl.when(p < 2)
        def _():
            give(rb, jnp.minimum(p, 1))

        @pl.when(p == 2)
        def _():
            give(out, 0)

        @pl.when(p == 0)
        def _():
            second = jnp.where(me < 63, 129 + me, jnp.where(me < 126, 66 + me, (me - 126) * (NG // 2)))
            fill_window(second, 1, win)

        return carry

    lax.fori_loop(0, 3, one_plane, 0)
    for p in range(2):
        part = rb.at[p, pl.ds(0, DEV - 1)]
        pltpu.make_async_copy(part, part, ry.at[p]).wait()
    for i, (p, c) in enumerate(((0, 0), (0, 1), (1, 0), (1, 1))):
        hi, lo = cut(rb[p, :, 0, c * CELLS : (c + 1) * CELLS])
        at = (i % 3) * DEV
        if i < 3:
            stack[at : at + DEV, :] = hi
            stack[NG + at : NG + at + DEV, :] = lo
            stack[2 * NG + at : 2 * NG + at + DEV, :] = hi
        if i == 2:
            ga[...] = mm(back[...], stack[...], NN)
        if i == 3:
            cols = slice(2 * DEV, 3 * DEV)
            fa[...] = (mm(back[:, cols], hi, NN) + mm(back[:, cols], lo, NN)) + mm(back[:, 2 * NG + 2 * DEV :], hi, NN)
    stores = [pltpu.make_async_copy(ga, ga_hbm, sl.at[0]), pltpu.make_async_copy(fa, fa_hbm, sl.at[1])]
    for c in stores:
        c.start()
    part = send.at[pl.ds(0, 15)]
    pltpu.make_async_copy(part, part, ss).wait()
    part = xg.at[pl.ds(0, DEV - 1)]
    pltpu.make_async_copy(part, part, sg).wait()
    for g in range(3):
        part = xf.at[g, pl.ds(0, DEV - 1)]
        pltpu.make_async_copy(part, part, sf.at[g]).wait()
    for p in range(3):
        part = ys.at[p, pl.ds(0, DEV - 1)]
        pltpu.make_async_copy(part, part, sy.at[p]).wait()
    for c in stores:
        c.wait()
    part = out.at[0, pl.ds(0, DEV - 1)]
    pltpu.make_async_copy(part, part, ry.at[2]).wait()


def last_body(r_hbm, ga_hbm, fa_hbm, table_hbm, out_hbm, r, ga, fa, table, stack, out, sem, done):
    loads = [
        pltpu.make_async_copy(a, b, sem.at[i])
        for i, (a, b) in enumerate(((r_hbm.at[0], r), (table_hbm, table), (fa_hbm, fa), (ga_hbm, ga)))
    ]
    for c in loads:
        c.start()
    loads[0].wait()
    for c in range(2):
        hi, lo = cut(r[:, 0, c * CELLS : (c + 1) * CELLS])
        at = c * DEV
        stack[at : at + DEV, :] = hi
        stack[2 * DEV + at : 2 * DEV + at + DEV, :] = lo
        stack[4 * DEV + at : 4 * DEV + at + DEV, :] = hi
    loads[1].wait()
    left = jnp.concatenate([table[:, i * NG : i * NG + 2 * DEV] for i in range(3)], axis=1)
    stores = []
    for xh in range(3):
        whole = slice(xh * NG, (xh + 1) * NG)
        f = mm(left, stack[:, whole], NN)
        if xh == 0:
            for c in loads[2:]:
                c.wait()
        f = fa[:, whole] + f
        frac = jnp.clip(f / jnp.maximum(ga[:, whole], 0.5), 0.0, 1.0)
        for lh in range(3):
            turned = frac[:, lh * 128 : (lh + 1) * 128].T
            for xl in range(16):
                at = (16 * xh + xl) * 24 + 8 * lh
                out[at : at + 8, :] = turned[xl * 8 : xl * 8 + 8, :]
        c = pltpu.make_async_copy(out.at[pl.ds(xh * NG, NG)], out_hbm.at[pl.ds(xh * NG, NG)], done.at[xh])
        c.start()
        stores.append(c)
    for c in stores:
        c.wait()


def sds(*shape, dtype=F32):
    return jax.ShapeDtypeStruct(shape, dtype)


def whole(halos, density, ahead, tw, back, mats):
    dma = pltpu.SemaphoreType.DMA
    plane = (DEV, 1, PLANE)
    anywhere, here = pl.BlockSpec(memory_space=pl.ANY), pl.BlockSpec(memory_space=VMEM)
    return pl.pallas_call(
        whole_body,
        out_shape=(sds(1, *plane), sds(NG, CELLS), sds(NG, CELLS)),
        in_specs=[here] * 4 + [anywhere] * 4 + [here] * 8,
        out_specs=(anywhere,) * 3,
        scratch_shapes=[
            VMEM((CELLS, NG), F32),
            VMEM((NG, 3 * NG), BF16),
            VMEM((16, 2 * CAP, SLOTS), F32),
            VMEM((16, 2 * CAP, SLOTS), F32),
            VMEM((2 * NG, 16 * CAP * SLOTS), BF16),
            VMEM((16 * CAP, SLOTS), jnp.int32),
            VMEM((NG, STEP), BF16),
            VMEM((NG, NG), F32),
            VMEM((3 * NG, NG), BF16),
            VMEM((DEV, 1, HALF), F32),
            VMEM((3, DEV, 1, CELLS), F32),
            VMEM((DEV, 1, HALF), F32),
            VMEM((3, DEV, 1, CELLS), F32),
            VMEM((3, *plane), F32),
            VMEM((2, *plane), F32),
            VMEM((2, CELLS, 128), F32),
            VMEM((4, CELLS, 128), F32),
            VMEM((NG, 3 * NG), BF16),
            VMEM((NG, CELLS), F32),
            VMEM((NG, CELLS), F32),
            VMEM((3 * NG, CELLS), BF16),
            VMEM((256, CELLS), F32),
            VMEM((CELLS, 256), F32),
            VMEM((CELLS, 256), BF16),
            VMEM((CELLS, 256), BF16),
            VMEM((256, CELLS), BF16),
            VMEM((256, CELLS), BF16),
            dma,
            dma,
            dma,
            dma,
            dma((3,)),
            dma((3,)),
            dma((3,)),
            dma((3,)),
            dma,
            dma((4,)),
        ],
        compiler_params=pltpu.CompilerParams(vmem_limit_bytes=63 << 20, collective_id=1, has_side_effects=True),
        cost_estimate=pl.CostEstimate(flops=36 << 30, bytes_accessed=8 << 20, transcendentals=0),
        name="whole",
    )(*halos, density, ahead, tw, back, *mats)


def on_device(photons, halo_cells, halo_counts, owners, density):
    table = z_table()
    ahead, back = stacked(table, 1), stacked(table.T, 1)
    mats = []
    for m in (row_matrix(1), row_matrix(-1), lane_matrix(1), lane_matrix(-1)):
        mats += [jnp.asarray(t) for t in cut_np(m)]

    dma = pltpu.SemaphoreType.DMA
    halos = (photons, halo_cells, halo_counts.reshape(1, 32), owners.reshape(1, 32))
    r, ga, fa = whole(halos, density.reshape(CELLS, NG), ahead, jnp.asarray(twiddles()), back, mats)
    anywhere = pl.BlockSpec(memory_space=pl.ANY)
    out = pl.pallas_call(
        last_body,
        out_shape=sds(CELLS, NG),
        in_specs=[anywhere] * 4,
        out_specs=anywhere,
        scratch_shapes=[VMEM((DEV, 1, PLANE), F32), VMEM((NG, CELLS), F32), VMEM((NG, CELLS), F32)]
        + [VMEM((NG, 3 * NG), BF16), VMEM((6 * DEV, CELLS), BF16), VMEM((CELLS, NG), F32), dma((4,)), dma((3,))],
        compiler_params=pltpu.CompilerParams(vmem_limit_bytes=LIMIT),
        cost_estimate=pl.CostEstimate(flops=1 << 30, bytes_accessed=6 << 20, transcendentals=0),
        name="last",
    )(r, ga, fa, back)
    return out.reshape(48, 24, NG)


def solution(mesh):
    placed = (
        P(("px", "py"), None),
        P(("px", "py"), None),
        P(("px", "py")),
        P(("px", "py"), None),
        P("px", "py", None),
    )
    return jax.shard_map(
        on_device, mesh=mesh, in_specs=placed, out_specs=P("px", "py", None), check_vma=False
    )
```

time: 129 us -> 115 us (0.89)
  Pallas kernels: 95.9 us -> 114 us
  starting transfers between devices: 16 us -> 0 us
  waiting for transfers between devices: 15.3 us -> 0 us
  local copies, waits for them, and re-layouts: 1.82 us -> 0 us
    pallas_call x5 -> x2, Pallas kernels: 95.9 us -> 114 us  [the longest x1 107 us: whole(): pl.pallas_call(whole_body, out_shape=(sds(1, *plane), sds(NG, CELLS), sds...]
    all_to_all x2 -> x0, starting transfers between devices: 16 us -> none  [the longest x1 9.45 us: on_device(): got = lax.all_to_all(send, 'py', split_axis=0, concat_axis=0, tiled=True)]
    all_to_all x2 -> x0, waiting for transfers between devices: 15.3 us -> none  [the longest x1 12.5 us: exchange(): lax.all_to_all(a, ('px', 'py'), split_axis=0, concat_axis=0, tiled=True)]
    unnamed x4 -> x0, local copies, waits for them, and re-layouts: 1.82 us -> none
  transfers between devices with their start and end apart: 2 -> 0, of which waited for: 2 -> 0; matrix products, arithmetic and copies ran while one was open for 0% -> 0% of each run, Pallas kernels for 15% -> 0%
where the time goes in v4:
time: 115 us
  Pallas kernels  114 us (99%)
    pallas_call x1, Pallas kernels, whole(): pl.pallas_call(whole_body, out_shape=(sds(1, *plane), sds(NG, CELLS), sds...  107 us
    pallas_call x1, Pallas kernels, on_device(): pl.pallas_call(last_body, out_shape=sds(CELLS, NG), in_specs=[anywhere] *...  7.05 us

profile of v4, /device:TPU:1, one launch (start us, length us, event | category | flops | bytes accessed | tf_op | source)
XLA Modules:
  0.0 114.5 jit_solution(363590985143664881)
XLA Ops:
  0.0 107.3 %whole.1 = (f32[1,128,1,2304]{3,2,1,0:T(1,128)}, f32[384,1152]{1,0:T(8,128)}, f32[384,1152]{1,0:T(8,128)}) custom-call(f32[32,128]{1,0:T(8,128)} %ph.1, s32[32,128]{1,0:T(8,128)} %cell.1, s32[1,32]{1,0:T(1,128)} %bitcast.5, s32[1,32]{1,0:T(1,128)} %bitcast.6, f32[1152,384]{1,0:T(8,128)} %bitcast.4, bf16[384,1152]{1,0:T(8,128)(2,1)} %constant.22.clone.table_hbm, ...), custom_call_target="tpu_custom_call" | custom-call | flops 38654705664 | bytes 8388608 | tf_op jit(solution)/shard_map/whole/pallas_call | solution.py:504
  107.3 7.0 %last.1 = f32[1152,384]{1,0:T(8,128)} custom-call(f32[1,128,1,2304]{3,2,1,0:T(1,128)} %get-tuple-element.8.r_hbm, f32[384,1152]{1,0:T(8,128)} %get-tuple-element.9.ga_hbm, f32[384,1152]{1,0:T(8,128)} %get-tuple-element.10.fa_hbm, bf16[384,1152]{1,0:T(8,128)(2,1)} %constant.23.clone.back_hbm.table_hbm), custom_call_target="tpu_custom_call" | custom-call | flops 1073741824 | bytes 6291456 | tf_op jit(solution)/shard_map/last/pallas_call | solution.py:565

commit v5 on v4

--- a/solution.py
+++ b/solution.py
@@ -190,27 +190,23 @@
 
 
 RB = 16
-def coords():
-    px, py = lax.axis_index("px"), lax.axis_index("py")
-    return px & 3, ((py >> 1) & 1) * 2 + (px >> 2), py >> 2, py & 1
-
-
-def partner(t):
-    x, y, z, core = coords()
-    u = (t * 101) & 127
-    sign = 1 - 2 * core
-    x2 = (x + sign * ((u >> 1) & 3)) & 3
-    y2 = (y + sign * ((u >> 3) & 3)) & 3
-    z2 = (z + sign * ((u >> 5) & 3)) & 3
-    return (y2 & 1) * 4 + x2, z2 * 4 + (y2 >> 1) * 2 + ((core + u) & 1)
+BATCH = 14
 
 
 def everyone(body):
-    def step(t, carry):
-        body(*partner(t))
+    me = lax.axis_index("px") * 16 + lax.axis_index("py")
+
+    def one(t):
+        other = me ^ ((t * 101) & (DEV - 1))
+        body(other, (other >> 4, other & 15))
+
+    def step(i, carry):
+        for u in range(BATCH):
+            one(1 + i * BATCH + u)
         return carry
 
-    lax.fori_loop(1, DEV, step, 0)
+    lax.fori_loop(0, (DEV - 2) // BATCH, step, 0)
+    one(DEV - 1)
 
 
 def fill_window(k, which, win):
@@ -233,8 +229,8 @@
 
 
 def whole_body(
-    ph, cell, count, owned, dens_hbm, table_hbm, tw_hbm, back_hbm, ah, al, bh, bl, ch, cl, dh, dl, out, ga_hbm, fa_hbm,
-    dens, table, send, land, zp, col, spread, acc, f3, xg, xf, gs, fs,
+    ph, cell, count, owned, dens_hbm, table_hbm, tw_hbm, back_hbm, ah, al, bh, bl, ch, cl, dh, dl, result,
+    dens, table, send, land, zp, col, spread, acc, f3, xg, xf, gs, fs, out,
     ys, rb, win, tw, back, ga, fa, stack, wide, tall, uh, ul, vh, vl, ss, rs, sg, rg, sf, rf, sy, ry, own, sl,
 ):
     px, py = lax.axis_index("px"), lax.axis_index("py")
@@ -246,11 +242,10 @@
     for c in loads:
         c.start()
     barrier = pltpu.get_barrier_semaphore()
-    everyone(lambda a, b: pl.semaphore_signal(barrier, inc=1, device_id=(a, b), device_id_type=MESH))
+    everyone(lambda i, to: pl.semaphore_signal(barrier, inc=1, device_id=to, device_id_type=MESH))
     send[...] = pack(ph[...], cell[...], count[...], owned[...])
-    mine = pltpu.make_async_copy(send.at[py], land.at[py], own)
-    mine.start()
-    mine.wait()
+    halo_own = pltpu.make_async_copy(send.at[py], land.at[py], own.at[0])
+    halo_own.start()
     loads[0].wait()
     for m in range(9):
         xh, lh = m // 3, m % 3
@@ -275,19 +270,20 @@
     res = mm(table[...], stack[...], NT)
     for c in range(3):
         xg[:, 0, c * CELLS : (c + 1) * CELLS] = res[c * DEV : (c + 1) * DEV]
-    mine = pltpu.make_async_copy(xg.at[me], gs.at[me], own)
-    mine.start()
-    mine.wait()
+    density_own = pltpu.make_async_copy(xg.at[me], gs.at[me], own.at[1])
+    density_own.start()
     everyone(
-        lambda a, b: pltpu.make_async_remote_copy(
-            src_ref=xg.at[a * 16 + b],
+        lambda i, to: pltpu.make_async_remote_copy(
+            src_ref=xg.at[i],
             dst_ref=gs.at[me],
             send_sem=sg,
             recv_sem=rg,
-            device_id=(a, b),
+            device_id=to,
             device_id_type=MESH,
         ).start()
     )
+    fill_window(me + 1, 0, win)
+    halo_own.wait()
     part = land.at[pl.ds(0, 15)]
     pltpu.make_async_copy(part, part, rs).wait()
     one_hots(land, zp, col)
@@ -301,23 +297,21 @@
         res = mm(table[...], f3[...], NN)
         for c, first in enumerate((2 * DEV, 0, DEV)):
             xf[g, :, 0, c * NG : (c + 1) * NG] = res[first : first + DEV]
-        mine = pltpu.make_async_copy(xf.at[g, me], fs.at[g, me], own)
-        mine.start()
-        mine.wait()
+        pltpu.make_async_copy(xf.at[g, me], fs.at[g, me], own.at[2 + g]).start()
         everyone(
-            lambda a, b: pltpu.make_async_remote_copy(
-                src_ref=xf.at[g, a * 16 + b],
+            lambda i, to: pltpu.make_async_remote_copy(
+                src_ref=xf.at[g, i],
                 dst_ref=fs.at[g, me],
                 send_sem=sf.at[g],
                 recv_sem=rf.at[g],
-                device_id=(a, b),
+                device_id=to,
                 device_id_type=MESH,
             ).start()
         )
         return carry
 
     lax.fori_loop(0, 3, one_group, 0)
-    fill_window(me + 1, 0, win)
+    density_own.wait()
     for c in loads[2:]:
         c.wait()
     part = gs.at[pl.ds(0, DEV - 1)]
@@ -332,6 +326,7 @@
         @pl.when(p == 1)
         def _():
             for g in range(3):
+                pltpu.make_async_copy(xf.at[g, me], fs.at[g, me], own.at[2 + g]).wait()
                 part = fs.at[g, pl.ds(0, DEV - 1)]
                 pltpu.make_async_copy(part, part, rf.at[g]).wait()
             wide[:DEV, :] = gs[:, 0, 2 * CELLS :]
@@ -391,28 +386,17 @@
         back = mm3(bh[...], bl[...], vh[...], vl[...])
         for c in range(2):
             ys[p, :, 0, c * CELLS : (c + 1) * CELLS] = back[c * DEV : (c + 1) * DEV]
-        def give(home, q):
-            mine = pltpu.make_async_copy(ys.at[p, me], home.at[q, me], own)
-            mine.start()
-            mine.wait()
-            everyone(
-                lambda a, b: pltpu.make_async_remote_copy(
-                    src_ref=ys.at[p, a * 16 + b],
-                    dst_ref=home.at[q, me],
-                    send_sem=sy.at[p],
-                    recv_sem=ry.at[p],
-                    device_id=(a, b),
-                    device_id_type=MESH,
-                ).start()
-            )
-
-        @pl.when(p < 2)
-        def _():
-            give(rb, jnp.minimum(p, 1))
-
-        @pl.when(p == 2)
-        def _():
-            give(out, 0)
+        pltpu.make_async_copy(ys.at[p, me], rb.at[p, me], own.at[5 + p]).start()
+        everyone(
+            lambda i, to: pltpu.make_async_remote_copy(
+                src_ref=ys.at[p, i],
+                dst_ref=rb.at[p, me],
+                send_sem=sy.at[p],
+                recv_sem=ry.at[p],
+                device_id=to,
+                device_id_type=MESH,
+            ).start()
+        )
 
         @pl.when(p == 0)
         def _():
@@ -423,10 +407,13 @@
 
     lax.fori_loop(0, 3, one_plane, 0)
     for p in range(2):
+        pltpu.make_async_copy(ys.at[p, me], rb.at[p, me], own.at[5 + p]).wait()
         part = rb.at[p, pl.ds(0, DEV - 1)]
         pltpu.make_async_copy(part, part, ry.at[p]).wait()
     for i, (p, c) in enumerate(((0, 0), (0, 1), (1, 0), (1, 1))):
-        hi, lo = cut(rb[p, :, 0, c * CELLS : (c + 1) * CELLS])
+        spot = (i % 2) * DEV
+        wide[spot : spot + DEV, :] = rb[p, :, 0, c * CELLS : (c + 1) * CELLS]
+        hi, lo = cut(wide[spot : spot + DEV, :])
         at = (i % 3) * DEV
         if i < 3:
             stack[at : at + DEV, :] = hi
@@ -437,9 +424,6 @@
         if i == 3:
             cols = slice(2 * DEV, 3 * DEV)
             fa[...] = (mm(back[:, cols], hi, NN) + mm(back[:, cols], lo, NN)) + mm(back[:, 2 * NG + 2 * DEV :], hi, NN)
-    stores = [pltpu.make_async_copy(ga, ga_hbm, sl.at[0]), pltpu.make_async_copy(fa, fa_hbm, sl.at[1])]
-    for c in stores:
-        c.start()
     part = send.at[pl.ds(0, 15)]
     pltpu.make_async_copy(part, part, ss).wait()
     part = xg.at[pl.ds(0, DEV - 1)]
@@ -450,43 +434,28 @@
     for p in range(3):
         part = ys.at[p, pl.ds(0, DEV - 1)]
         pltpu.make_async_copy(part, part, sy.at[p]).wait()
-    for c in stores:
-        c.wait()
-    part = out.at[0, pl.ds(0, DEV - 1)]
+    pltpu.make_async_copy(ys.at[2, me], rb.at[2, me], own.at[7]).wait()
+    part = rb.at[2, pl.ds(0, DEV - 1)]
     pltpu.make_async_copy(part, part, ry.at[2]).wait()
-
-
-def last_body(r_hbm, ga_hbm, fa_hbm, table_hbm, out_hbm, r, ga, fa, table, stack, out, sem, done):
-    loads = [
-        pltpu.make_async_copy(a, b, sem.at[i])
-        for i, (a, b) in enumerate(((r_hbm.at[0], r), (table_hbm, table), (fa_hbm, fa), (ga_hbm, ga)))
-    ]
-    for c in loads:
-        c.start()
-    loads[0].wait()
     for c in range(2):
-        hi, lo = cut(r[:, 0, c * CELLS : (c + 1) * CELLS])
         at = c * DEV
+        wide[at : at + DEV, :] = rb[2, :, 0, c * CELLS : (c + 1) * CELLS]
+        hi, lo = cut(wide[at : at + DEV, :])
         stack[at : at + DEV, :] = hi
         stack[2 * DEV + at : 2 * DEV + at + DEV, :] = lo
         stack[4 * DEV + at : 4 * DEV + at + DEV, :] = hi
-    loads[1].wait()
-    left = jnp.concatenate([table[:, i * NG : i * NG + 2 * DEV] for i in range(3)], axis=1)
+    left = jnp.concatenate([back[:, i * NG : i * NG + 2 * DEV] for i in range(3)], axis=1)
     stores = []
     for xh in range(3):
-        whole = slice(xh * NG, (xh + 1) * NG)
-        f = mm(left, stack[:, whole], NN)
-        if xh == 0:
-            for c in loads[2:]:
-                c.wait()
-        f = fa[:, whole] + f
-        frac = jnp.clip(f / jnp.maximum(ga[:, whole], 0.5), 0.0, 1.0)
+        cols = slice(xh * NG, (xh + 1) * NG)
+        f = fa[:, cols] + mm(left, stack[: 6 * DEV, cols], NN)
+        frac = jnp.clip(f / jnp.maximum(ga[:, cols], 0.5), 0.0, 1.0)
         for lh in range(3):
             turned = frac[:, lh * 128 : (lh + 1) * 128].T
             for xl in range(16):
                 at = (16 * xh + xl) * 24 + 8 * lh
                 out[at : at + 8, :] = turned[xl * 8 : xl * 8 + 8, :]
-        c = pltpu.make_async_copy(out.at[pl.ds(xh * NG, NG)], out_hbm.at[pl.ds(xh * NG, NG)], done.at[xh])
+        c = pltpu.make_async_copy(out.at[pl.ds(xh * NG, NG)], result.at[pl.ds(xh * NG, NG)], sl.at[xh])
         c.start()
         stores.append(c)
     for c in stores:
@@ -503,9 +472,9 @@
     anywhere, here = pl.BlockSpec(memory_space=pl.ANY), pl.BlockSpec(memory_space=VMEM)
     return pl.pallas_call(
         whole_body,
-        out_shape=(sds(1, *plane), sds(NG, CELLS), sds(NG, CELLS)),
+        out_shape=sds(CELLS, NG),
         in_specs=[here] * 4 + [anywhere] * 4 + [here] * 8,
-        out_specs=(anywhere,) * 3,
+        out_specs=anywhere,
         scratch_shapes=[
             VMEM((CELLS, NG), F32),
             VMEM((NG, 3 * NG), BF16),
@@ -520,8 +489,9 @@
             VMEM((3, DEV, 1, CELLS), F32),
             VMEM((DEV, 1, HALF), F32),
             VMEM((3, DEV, 1, CELLS), F32),
+            VMEM((CELLS, NG), F32),
             VMEM((3, *plane), F32),
-            VMEM((2, *plane), F32),
+            VMEM((3, *plane), F32),
             VMEM((2, CELLS, 128), F32),
             VMEM((4, CELLS, 128), F32),
             VMEM((NG, 3 * NG), BF16),
@@ -542,7 +512,7 @@
             dma((3,)),
             dma((3,)),
             dma((3,)),
-            dma,
+            dma((8,)),
             dma((4,)),
         ],
         compiler_params=pltpu.CompilerParams(vmem_limit_bytes=63 << 20, collective_id=1, has_side_effects=True),
@@ -558,21 +528,8 @@
     for m in (row_matrix(1), row_matrix(-1), lane_matrix(1), lane_matrix(-1)):
         mats += [jnp.asarray(t) for t in cut_np(m)]
 
-    dma = pltpu.SemaphoreType.DMA
     halos = (photons, halo_cells, halo_counts.reshape(1, 32), owners.reshape(1, 32))
-    r, ga, fa = whole(halos, density.reshape(CELLS, NG), ahead, jnp.asarray(twiddles()), back, mats)
-    anywhere = pl.BlockSpec(memory_space=pl.ANY)
-    out = pl.pallas_call(
-        last_body,
-        out_shape=sds(CELLS, NG),
-        in_specs=[anywhere] * 4,
-        out_specs=anywhere,
-        scratch_shapes=[VMEM((DEV, 1, PLANE), F32), VMEM((NG, CELLS), F32), VMEM((NG, CELLS), F32)]
-        + [VMEM((NG, 3 * NG), BF16), VMEM((6 * DEV, CELLS), BF16), VMEM((CELLS, NG), F32), dma((4,)), dma((3,))],
-        compiler_params=pltpu.CompilerParams(vmem_limit_bytes=LIMIT),
-        cost_estimate=pl.CostEstimate(flops=1 << 30, bytes_accessed=6 << 20, transcendentals=0),
-        name="last",
-    )(r, ga, fa, back)
+    out = whole(halos, density.reshape(CELLS, NG), ahead, jnp.asarray(twiddles()), back, mats)
     return out.reshape(48, 24, NG)
 
 

time: 115 us -> 104 us (0.904)
  Pallas kernels: 114 us -> 101 us
  local copies, waits for them, and re-layouts: 0 us -> 2.8 us
    pallas_call x2 -> x1, Pallas kernels: 114 us -> 101 us  [whole(): pl.pallas_call(whole_body, out_shape=sds(CELLS, NG), in_specs=[here] * 4...]
    unnamed x0 -> x1, local copies, waits for them, and re-layouts: none -> 2.8 us
where the time goes in v5:
time: 104 us
  Pallas kernels  101 us (97%)
  local copies, waits for them, and re-layouts  2.8 us (3%)
    pallas_call x1, Pallas kernels, whole(): pl.pallas_call(whole_body, out_shape=sds(CELLS, NG), in_specs=[here] * 4...  101 us
    unnamed x1, local copies, waits for them, and re-layouts  2.8 us

profile of v5, /device:TPU:1, one launch (start us, length us, event | category | flops | bytes accessed | tf_op | source)
XLA Modules:
  0.0 103.9 jit_solution(15736422898812822878)
XLA Ops:
  0.0 101.1 %whole.1 = f32[1152,384]{1,0:T(8,128)} custom-call(f32[32,128]{1,0:T(8,128)} %ph.1, s32[32,128]{1,0:T(8,128)} %cell.1, s32[1,32]{1,0:T(1,128)} %bitcast.6, s32[1,32]{1,0:T(1,128)} %bitcast.7, f32[1152,384]{1,0:T(8,128)} %bitcast.5, bf16[384,1152]{1,0:T(8,128)(2,1)} %constant.22.clone.table_hbm, f32[4,1152,128]{2,1,0:T(8,128)} %constant.32.clone.tw_hbm, ...), custom_call_target="tpu_custom_call" | custom-call | flops 38654705664 | bytes 8388608 | tf_op jit(solution)/shard_map/whole/pallas_call | solution.py:473
  101.1 2.8 %copy.18 = f32[48,24,384]{2,1,0:T(8,128)} copy(f32[48,24,384]{2,1,0:T(8,128)} %bitcast.4) | data formatting | bytes 3538944

commit v6 on v5

--- a/solution.py
+++ b/solution.py
@@ -229,20 +229,22 @@
 
 
 def whole_body(
-    ph, cell, count, owned, dens_hbm, table_hbm, tw_hbm, back_hbm, ah, al, bh, bl, ch, cl, dh, dl, result,
+    ph, cell, count, owned, dens_hbm, table_hbm, tw_hbm, back_hbm, mats_hbm, result,
     dens, table, send, land, zp, col, spread, acc, f3, xg, xf, gs, fs, out,
-    ys, rb, win, tw, back, ga, fa, stack, wide, tall, uh, ul, vh, vl, ss, rs, sg, rg, sf, rf, sy, ry, own, sl,
+    ys, rb, win, tw, back, ga, fa, mats, stack, wide, tall, uh, ul, vh, vl, ss, rs, sg, rg, sf, rf, sy, ry, own, sl,
 ):
     px, py = lax.axis_index("px"), lax.axis_index("py")
     me = px * 16 + py
     loads = [
         pltpu.make_async_copy(a, b, sl.at[i])
-        for i, (a, b) in enumerate(((dens_hbm, dens), (table_hbm, table), (tw_hbm, tw), (back_hbm, back)))
+        for i, (a, b) in enumerate(((dens_hbm, dens), (table_hbm, table), (tw_hbm, tw), (back_hbm, back), (mats_hbm, mats)))
     ]
-    for c in loads:
-        c.start()
+    ah, al, bh, bl, ch, cl, dh, dl = (mats.at[i] for i in range(8))
+    loads[0].start()
     barrier = pltpu.get_barrier_semaphore()
     everyone(lambda i, to: pl.semaphore_signal(barrier, inc=1, device_id=to, device_id_type=MESH))
+    for c in loads[1:]:
+        c.start()
     send[...] = pack(ph[...], cell[...], count[...], owned[...])
     halo_own = pltpu.make_async_copy(send.at[py], land.at[py], own.at[0])
     halo_own.start()
@@ -385,18 +387,37 @@
         lax.fori_loop(0, DEV // RB, backward, 0)
         back = mm3(bh[...], bl[...], vh[...], vl[...])
         for c in range(2):
-            ys[p, :, 0, c * CELLS : (c + 1) * CELLS] = back[c * DEV : (c + 1) * DEV]
+            for g in range(3):
+                at = (2 * g + c) * NG
+                ys[p, :, 0, at : at + NG] = back[c * DEV : (c + 1) * DEV, g * NG : (g + 1) * NG]
         pltpu.make_async_copy(ys.at[p, me], rb.at[p, me], own.at[5 + p]).start()
-        everyone(
-            lambda i, to: pltpu.make_async_remote_copy(
-                src_ref=ys.at[p, i],
-                dst_ref=rb.at[p, me],
-                send_sem=sy.at[p],
-                recv_sem=ry.at[p],
-                device_id=to,
-                device_id_type=MESH,
-            ).start()
-        )
+        @pl.when(p < 2)
+        def _():
+            everyone(
+                lambda i, to: pltpu.make_async_remote_copy(
+                    src_ref=ys.at[p, i],
+                    dst_ref=rb.at[p, me],
+                    send_sem=sy.at[p],
+                    recv_sem=ry.at[p],
+                    device_id=to,
+                    device_id_type=MESH,
+                ).start()
+            )
+
+        @pl.when(p == 2)
+        def _():
+            for g in range(3):
+                cols = pl.ds(2 * g * NG, 2 * NG)
+                everyone(
+                    lambda i, to: pltpu.make_async_remote_copy(
+                        src_ref=ys.at[2, i, :, cols],
+                        dst_ref=rb.at[2, me, :, cols],
+                        send_sem=sy.at[2 + g],
+                        recv_sem=ry.at[2 + g],
+                        device_id=to,
+                        device_id_type=MESH,
+                    ).start()
+                )
 
         @pl.when(p == 0)
         def _():
@@ -412,7 +433,8 @@
         pltpu.make_async_copy(part, part, ry.at[p]).wait()
     for i, (p, c) in enumerate(((0, 0), (0, 1), (1, 0), (1, 1))):
         spot = (i % 2) * DEV
-        wide[spot : spot + DEV, :] = rb[p, :, 0, c * CELLS : (c + 1) * CELLS]
+        for g in range(3):
+            wide[spot : spot + DEV, g * NG : (g + 1) * NG] = rb[p, :, 0, (2 * g + c) * NG : (2 * g + c + 1) * NG]
         hi, lo = cut(wide[spot : spot + DEV, :])
         at = (i % 3) * DEV
         if i < 3:
@@ -431,23 +453,23 @@
     for g in range(3):
         part = xf.at[g, pl.ds(0, DEV - 1)]
         pltpu.make_async_copy(part, part, sf.at[g]).wait()
-    for p in range(3):
+    for p in range(2):
         part = ys.at[p, pl.ds(0, DEV - 1)]
         pltpu.make_async_copy(part, part, sy.at[p]).wait()
     pltpu.make_async_copy(ys.at[2, me], rb.at[2, me], own.at[7]).wait()
-    part = rb.at[2, pl.ds(0, DEV - 1)]
-    pltpu.make_async_copy(part, part, ry.at[2]).wait()
-    for c in range(2):
-        at = c * DEV
-        wide[at : at + DEV, :] = rb[2, :, 0, c * CELLS : (c + 1) * CELLS]
-        hi, lo = cut(wide[at : at + DEV, :])
-        stack[at : at + DEV, :] = hi
-        stack[2 * DEV + at : 2 * DEV + at + DEV, :] = lo
-        stack[4 * DEV + at : 4 * DEV + at + DEV, :] = hi
     left = jnp.concatenate([back[:, i * NG : i * NG + 2 * DEV] for i in range(3)], axis=1)
     stores = []
     for xh in range(3):
         cols = slice(xh * NG, (xh + 1) * NG)
+        part = rb.at[2, pl.ds(0, DEV - 1), :, pl.ds(2 * xh * NG, 2 * NG)]
+        pltpu.make_async_copy(part, part, ry.at[2 + xh]).wait()
+        for c in range(2):
+            at = c * DEV
+            wide[at : at + DEV, cols] = rb[2, :, 0, (2 * xh + c) * NG : (2 * xh + c + 1) * NG]
+            hi, lo = cut(wide[at : at + DEV, cols])
+            stack[at : at + DEV, cols] = hi
+            stack[2 * DEV + at : 2 * DEV + at + DEV, cols] = lo
+            stack[4 * DEV + at : 4 * DEV + at + DEV, cols] = hi
         f = fa[:, cols] + mm(left, stack[: 6 * DEV, cols], NN)
         frac = jnp.clip(f / jnp.maximum(ga[:, cols], 0.5), 0.0, 1.0)
         for lh in range(3):
@@ -458,6 +480,9 @@
         c = pltpu.make_async_copy(out.at[pl.ds(xh * NG, NG)], result.at[pl.ds(xh * NG, NG)], sl.at[xh])
         c.start()
         stores.append(c)
+    for g in range(3):
+        part = ys.at[2, pl.ds(0, DEV - 1), :, pl.ds(2 * g * NG, 2 * NG)]
+        pltpu.make_async_copy(part, part, sy.at[2 + g]).wait()
     for c in stores:
         c.wait()
 
@@ -473,7 +498,7 @@
     return pl.pallas_call(
         whole_body,
         out_shape=sds(CELLS, NG),
-        in_specs=[here] * 4 + [anywhere] * 4 + [here] * 8,
+        in_specs=[here] * 4 + [anywhere] * 5,
         out_specs=anywhere,
         scratch_shapes=[
             VMEM((CELLS, NG), F32),
@@ -497,6 +522,7 @@
             VMEM((NG, 3 * NG), BF16),
             VMEM((NG, CELLS), F32),
             VMEM((NG, CELLS), F32),
+            VMEM((8, 256, 256), BF16),
             VMEM((3 * NG, CELLS), BF16),
             VMEM((256, CELLS), F32),
             VMEM((CELLS, 256), F32),
@@ -510,15 +536,15 @@
             dma,
             dma((3,)),
             dma((3,)),
-            dma((3,)),
-            dma((3,)),
+            dma((5,)),
+            dma((5,)),
             dma((8,)),
-            dma((4,)),
+            dma((5,)),
         ],
         compiler_params=pltpu.CompilerParams(vmem_limit_bytes=63 << 20, collective_id=1, has_side_effects=True),
         cost_estimate=pl.CostEstimate(flops=36 << 30, bytes_accessed=8 << 20, transcendentals=0),
         name="whole",
-    )(*halos, density, ahead, tw, back, *mats)
+    )(*halos, density, ahead, tw, back, mats)
 
 
 def on_device(photons, halo_cells, halo_counts, owners, density):
@@ -526,7 +552,8 @@
     ahead, back = stacked(table, 1), stacked(table.T, 1)
     mats = []
     for m in (row_matrix(1), row_matrix(-1), lane_matrix(1), lane_matrix(-1)):
-        mats += [jnp.asarray(t) for t in cut_np(m)]
+        mats += cut_np(m)
+    mats = jnp.asarray(np.stack(mats))
 
     halos = (photons, halo_cells, halo_counts.reshape(1, 32), owners.reshape(1, 32))
     out = whole(halos, density.reshape(CELLS, NG), ahead, jnp.asarray(twiddles()), back, mats)

time: 104 us -> 103 us (level)
  Pallas kernels: 101 us -> 99.6 us
    pallas_call x1, Pallas kernels: 101 us -> 99.6 us  [whole(): pl.pallas_call(whole_body, out_shape=sds(CELLS, NG), in_specs=[here] * 4...]
where the time goes in v6:
time: 103 us; the launch traced here: 102 us
  Pallas kernels  99.6 us (97%)
  local copies, waits for them, and re-layouts  2.8 us (3%)
    pallas_call x1, Pallas kernels, whole(): pl.pallas_call(whole_body, out_shape=sds(CELLS, NG), in_specs=[here] * 4...  99.6 us
    unnamed x1, local copies, waits for them, and re-layouts  2.8 us

profile of v6, /device:TPU:1, one launch (start us, length us, event | category | flops | bytes accessed | tf_op | source)
XLA Modules:
  0.0 102.4 jit_solution(10950161784026504279)
XLA Ops:
  0.0 99.6 %whole.1 = f32[1152,384]{1,0:T(8,128)} custom-call(f32[32,128]{1,0:T(8,128)} %ph.1, s32[32,128]{1,0:T(8,128)} %cell.1, s32[1,32]{1,0:T(1,128)} %bitcast.6, s32[1,32]{1,0:T(1,128)} %bitcast.7, f32[1152,384]{1,0:T(8,128)} %bitcast.5, bf16[384,1152]{1,0:T(8,128)(2,1)} %constant.8.clone.table_hbm, f32[4,1152,128]{2,1,0:T(8,128)} %constant.11.clone.tw_hbm, ...), custom_call_target="tpu_custom_call" | custom-call | flops 38654705664 | bytes 8388608 | tf_op jit(solution)/shard_map/whole/pallas_call | solution.py:498
  99.6 2.8 %copy.11 = f32[48,24,384]{2,1,0:T(8,128)} copy(f32[48,24,384]{2,1,0:T(8,128)} %bitcast.4) | data formatting | bytes 3538944

commit v7 on v6

--- a/solution.py
+++ b/solution.py
@@ -284,7 +284,6 @@
             device_id_type=MESH,
         ).start()
     )
-    fill_window(me + 1, 0, win)
     halo_own.wait()
     part = land.at[pl.ds(0, 15)]
     pltpu.make_async_copy(part, part, rs).wait()
@@ -313,6 +312,7 @@
         return carry
 
     lax.fori_loop(0, 3, one_group, 0)
+    fill_window(me + 1, 0, win)
     density_own.wait()
     for c in loads[2:]:
         c.wait()

time: 103 us -> 106 us (1.029)
  Pallas kernels: 99.6 us -> 103 us
    pallas_call x1, Pallas kernels: 99.6 us -> 103 us  [whole(): pl.pallas_call(whole_body, out_shape=sds(CELLS, NG), in_specs=[here] * 4...]
where the time goes in v7:
time: 106 us
  Pallas kernels  103 us (97%)
  local copies, waits for them, and re-layouts  2.8 us (3%)
    pallas_call x1, Pallas kernels, whole(): pl.pallas_call(whole_body, out_shape=sds(CELLS, NG), in_specs=[here] * 4...  103 us
    unnamed x1, local copies, waits for them, and re-layouts  2.8 us

profile of v7, /device:TPU:1, one launch (start us, length us, event | category | flops | bytes accessed | tf_op | source)
XLA Modules:
  0.0 105.6 jit_solution(12405068092412674602)
XLA Ops:
  0.0 102.8 %whole.1 = f32[1152,384]{1,0:T(8,128)} custom-call(f32[32,128]{1,0:T(8,128)} %ph.1, s32[32,128]{1,0:T(8,128)} %cell.1, s32[1,32]{1,0:T(1,128)} %bitcast.6, s32[1,32]{1,0:T(1,128)} %bitcast.7, f32[1152,384]{1,0:T(8,128)} %bitcast.5, bf16[384,1152]{1,0:T(8,128)(2,1)} %constant.8.clone.table_hbm, f32[4,1152,128]{2,1,0:T(8,128)} %constant.11.clone.tw_hbm, ...), custom_call_target="tpu_custom_call" | custom-call | flops 38654705664 | bytes 8388608 | tf_op jit(solution)/shard_map/whole/pallas_call | solution.py:498
  102.8 2.8 %copy.11 = f32[48,24,384]{2,1,0:T(8,128)} copy(f32[48,24,384]{2,1,0:T(8,128)} %bitcast.4) | data formatting | bytes 3538944
